TPU v7x, 256 devices: a whole 4x4x8 slice. The times are simulated.
256 devices in a mesh: samp: 32 (over z, y), pos: 8 (over x, core).
Axes of the slice: x: 4, y: 4, z: 8, core: 2. Of those that a mesh axis runs over, the one named last changes fastest.
Arguments:
- dosages: bfloat16 [65536, 4096], P('samp', 'pos')
- phenotypes: bfloat16 [65536, 2048], P('samp')
- gene_weights: bfloat16 [4096, 16], P('pos'), may hold values from -0.1875 to 0.1875
- gene_start: int32 [16], replicated, may hold values from 0 to 3072, as said below
- gene_end: int32 [16], replicated, may hold values from 1024 to 4096, as said below
Outputs:
- variant_z: float32 [2048, 4096], P('samp', 'pos')
- gene_z: float32 [2048, 16], P('samp', 'pos')
Inputs may be any that keep to these rules, and one draw needn't show every extreme that they name: gene_end - gene_start lies between 1024 and 2048; some window starts at 0 and some ends at 4096. gene_end is greater than gene_start of the same gene.
All inputs are finite; a program needn't handle non-finite values.
Results may differ from a plain program's by a relative error of at most 0.0029.
Values sent between devices are 32-bit elements; how exact they have to be, the bound alone decides.
No kernel may reach another device: no remote copies, remote signals or barrier semaphores. Data moves between devices by JAX's collectives and lax.ppermute only.
A program may use at most 64 MiB of HBM per device.

v0:
```python
import jax
import jax.numpy as jnp
from jax import lax
from jax.sharding import Mesh
from jax.sharding import PartitionSpec as P

SAMP = ("samp_0", "samp_1")


EPSILON = 1e-06


def sent_to_all(x, axis):
    copies = jnp.broadcast_to(x, (lax.axis_size(axis), *x.shape))
    return lax.all_to_all(copies, axis, split_axis=0, concat_axis=0, tiled=True)


def of_everyone(x, axis):
    return sent_to_all(x, axis).sum(axis=0)


def summed_rows(total, axes):
    for axis in axes:
        total = lax.psum_scatter(total, axis, scatter_dimension=0, tiled=True)
    return total


def cut_along(x, dim, count):
    before, after = (x.shape[:dim], x.shape[dim + 1 :])
    return jnp.moveaxis(x.reshape(*before, count, -1, *after), dim, 0)


def sum_at_owner(x, axis, dim):
    blocks = cut_along(x, dim, lax.axis_size(axis))
    arrived = lax.all_to_all(blocks, axis, split_axis=0, concat_axis=0, tiled=True)
    return arrived.sum(axis=0)


def packed_total(arrays, axis):
    line, at, outs = (jnp.concatenate([a.reshape(-1) for a in arrays]), 0, [])
    total = of_everyone(line, axis)
    for a in arrays:
        outs.append(total[at : at + a.size].reshape(a.shape))
        at += a.size
    return tuple(outs)


def contract(left, right):
    return lax.dot_general(
        left, right, (((0,), (0,)), ((), ())), preferred_element_type=jnp.float32
    )


def per_device(dosages, phenotypes, gene_weights, gene_start, gene_end):
    width_here = dosages.shape[1]
    gene_count = gene_weights.shape[1]
    gene_share = gene_count // lax.axis_size("pos")
    trait_share = phenotypes.shape[1] // lax.axis_size(SAMP)
    offset = lax.axis_index("pos") * width_here
    position = offset + lax.broadcasted_iota(jnp.int32, (width_here, gene_count), 0)
    inside = (position >= gene_start[None, :]) & (position < gene_end[None, :])
    masked = jnp.where(inside, gene_weights, jnp.zeros_like(gene_weights))
    partial_value = jnp.dot(dosages, masked, preferred_element_type=jnp.float32)
    summed = of_everyone(partial_value, "pos")
    predicted = lax.dynamic_slice_in_dim(summed, lax.axis_index("pos") * gene_share, gene_share, 1)
    pred_low = predicted.astype(jnp.bfloat16)
    samples = dosages.shape[0] * lax.axis_size(SAMP)
    dose_sq = jnp.sum(jnp.square(dosages.astype(jnp.float32)), axis=0)
    pred_sq = jnp.sum(predicted * predicted, axis=0)
    trait_sq = jnp.sum(jnp.square(phenotypes.astype(jnp.float32)), axis=0)
    marginal = summed_rows(contract(phenotypes, dosages), SAMP)
    gene_cross = sum_at_owner(contract(phenotypes, pred_low), SAMP, 0)
    dose_total, pred_total, trait_total = packed_total((dose_sq, pred_sq, trait_sq), SAMP)
    trait_own = lax.dynamic_slice_in_dim(
        trait_total, lax.axis_index(SAMP) * trait_share, trait_share, 0
    )
    mean_dose = dose_total / samples
    mean_pred = pred_total / samples
    mean_trait = trait_own / samples
    variant_z = marginal / jnp.sqrt(
        samples * (mean_trait[:, None] + EPSILON) * (mean_dose[None, :] + EPSILON)
    )
    gene_z = gene_cross / jnp.sqrt(
        samples * (mean_trait[:, None] + EPSILON) * (mean_pred[None, :] + EPSILON)
    )
    return (variant_z, gene_z)


def solution(mesh):
    finer = Mesh(mesh.devices.reshape(8, 4, mesh.shape["pos"]), ("samp_0", "samp_1", "pos"))
    in_specs = (P(SAMP, "pos"), P(SAMP, None), P("pos", None), P(), P())
    out_specs = (P(SAMP, "pos"), P(SAMP, "pos"))
    return jax.shard_map(
        per_device, mesh=finer, in_specs=in_specs, out_specs=out_specs, check_vma=False
    )
```

profile of v0, /device:TPU:2, one launch (start us, length us, event | category | flops | bytes accessed | tf_op | source)
XLA Modules:
  0.0 117.0 jit_solution(13675431724176723119)
XLA Ops:
  7.2 0.0 reduce-scatter.3.cloned.1.call-start
  7.2 10.5 %fusion.8 = f32[2048,512]{1,0:T(8,128)} fusion(bf16[2048,2048]{1,0:T(8,128)(2,1)} %param.6, bf16[2048,512]{1,0:T(8,128)(2,1)} %param.5), kind=kOutput, calls=%fused_computation.23 | convolution fusion | flops 4294967296 | bytes 14680064 | tf_op jit(solution)/shard_map/dot_general | solution.py:49
  17.7 0.0 reduce-scatter.3.cloned.1.call-update
  17.7 1.5 %copy-done = bf16[2048,512]{1,0:T(8,128)(2,1)S(1)} copy-done((bf16[2048,512]{1,0:T(8,128)(2,1)S(1)}, bf16[2048,512]{1,0:T(8,128)(2,1)}, u32[]{:S(2)}) %copy-start) | copy-done | bytes 2097176
  19.3 0.6 convolution_bitcast_fusion
  19.9 1.1 broadcast_in_dim.7
  21.0 5.7 %all-to-all-start = ((f32[8,2048,16]{1,2,0:T(8,128)}), f32[8,2048,16]{1,2,0:T(8,128)S(1)}, u32[]{:S(2)}, u32[]{:S(2)}) async-start(f32[8,2048,16]{1,2,0:T(8,128)} %broadcast_in_dim.7), calls=%async_computation.2 | async-start | bytes 2097152 | tf_op jit(solution)/shard_map/all_to_all | solution.py:15
  26.7 5.1 %multiply_reduce_fusion = f32[2048]{0:T(1024)S(1)} fusion(bf16[2048,2048]{1,0:T(8,128)(2,1)} %param.6), kind=kLoop, calls=%fused_computation | loop fusion | flops 12580864 | bytes 8396800 | tf_op jit(solution)/shard_map/reduce_sum | solution.py:70
  31.8 9.4 %all-to-all-done = f32[8,2048,16]{1,2,0:T(8,128)S(1)} async-done(((f32[8,2048,16]{1,2,0:T(8,128)}), f32[8,2048,16]{1,2,0:T(8,128)S(1)}, u32[]{:S(2)}, u32[]{:S(2)}) %all-to-all-start) | async-done | bytes 1048608 | tf_op jit(solution)/shard_map/all_to_all | solution.py:15
  41.2 0.1 reduce_sum.55
  41.3 4.7 %convolution_bitcast_fusion.1 = f32[2048,2]{0,1:T(2,128)S(1)} fusion(bf16[2048,2048]{1,0:T(8,128)(2,1)} %param.6, f32[2048,16]{0,1:T(8,128)S(1)} %reduce_sum.55, s32[]{:T(128)S(6)} %select_n.11), kind=kOutput, calls=%fused_computation.3 | convolution fusion | flops 16777216 | bytes 8413188 | tf_op jit(solution)/shard_map/dot_general | solution.py:49
  46.0 0.1 reshape.20
  46.1 0.7 reshape.21
  46.8 10.6 %all-to-all-start.2 = ((f32[32,1,128]{2,1,0:T(1,128)}), f32[32,1,128]{2,1,0:T(1,128)S(1)}, u32[]{:S(2)}, u32[]{:S(2)}) async-start(f32[32,1,128]{2,1,0:T(1,128)} %reshape.21), calls=%async_computation.4 | async-start | bytes 32768 | tf_op jit(solution)/shard_map/all_to_all | solution.py:35
  57.4 0.5 multiply_reduce_fusion.1
  57.9 0.1 multiply_reduce_fusion.2
  58.0 0.1 concatenate.3
  58.1 9.2 %all-to-all-done.2 = f32[32,1,128]{2,1,0:T(1,128)S(1)} async-done(((f32[32,1,128]{2,1,0:T(1,128)}), f32[32,1,128]{2,1,0:T(1,128)S(1)}, u32[]{:S(2)}, u32[]{:S(2)}) %all-to-all-start.2) | async-done | bytes 16416 | tf_op jit(solution)/shard_map/all_to_all | solution.py:35
  67.3 0.9 broadcast_in_dim.8
  68.2 3.9 %all-to-all-start.1 = ((f32[32,1,2562]{2,1,0:T(1,128)}), f32[32,1,2562]{2,1,0:T(1,128)S(1)}, u32[]{:S(2)}, u32[]{:S(2)}) async-start(f32[32,1,2562]{2,1,0:T(1,128)} %broadcast_in_dim.8), calls=%async_computation.3 | async-start | bytes 688128 | tf_op jit(solution)/shard_map/all_to_all | solution.py:15
  72.1 0.0 reduce-scatter.5.cloned.1.call-start
  72.2 5.3 %reduce-scatter.3.cloned.1.call-done = f32[256,512]{1,0:T(8,128)} async-done(((f32[2048,512]{1,0:T(8,128)}), f32[256,512]{1,0:T(8,128)}) %reduce-scatter.3.cloned.1.call-update) | async-done | bytes 524304 | tf_op jit(solution)/shard_map/reduce_scatter | solution.py:24
  77.5 0.5 broadcast.37
  78.0 0.7 reduce.1
  78.7 0.1 reshape.22
  78.9 7.2 %all-to-all-done.1 = f32[32,1,2562]{2,1,0:T(1,128)S(1)} async-done(((f32[32,1,2562]{2,1,0:T(1,128)}), f32[32,1,2562]{2,1,0:T(1,128)S(1)}, u32[]{:S(2)}, u32[]{:S(2)}) %all-to-all-start.1) | async-done | bytes 327968 | tf_op jit(solution)/shard_map/all_to_all | solution.py:15
  86.0 0.2 reduce_sum.58
  86.2 0.1 slice.12
  86.3 0.1 add_multiply_fusion
  86.4 0.6 rsqrt_multiply_fusion.1
  87.1 21.4 %reduce-scatter.5.cloned.1.call-done = f32[64,512]{1,0:T(8,128)} async-done(((f32[256,512]{1,0:T(8,128)}), f32[64,512]{1,0:T(8,128)}) %reduce-scatter.5.cloned.1.call-update) | async-done | bytes 131088 | tf_op jit(solution)/shard_map/reduce_scatter | solution.py:24
  108.5 1.7 %rsqrt_multiply_fusion = f32[64,512]{1,0:T(8,128)} fusion(f32[64,512]{1,0:T(8,128)} %reduce-scatter.5.cloned.1.call-done, f32[512]{0:T(512)S(1)} %fusion.4, f32[64]{0:T(128)S(1)} %add_multiply_fusion), kind=kLoop, calls=%fused_computation.4 | loop fusion | flops 65536 | bytes 264448 | tf_op jit(solution)/shard_map/div | solution.py:80
  (13 shorter events, 0.1 us)
Async XLA Ops:
  7.2 70.3 %reduce-scatter.3.cloned.1.call-start = ((), (), s32[]{:S(2)}) async-start(), calls=%async_computation.5 | async-start | bytes 4718592 | tf_op jit(solution)/shard_map/reduce_scatter | solution.py:24
  17.7 1.6 %copy-start = (bf16[2048,512]{1,0:T(8,128)(2,1)S(1)}, bf16[2048,512]{1,0:T(8,128)(2,1)}, u32[]{:S(2)}) copy-start(bf16[2048,512]{1,0:T(8,128)(2,1)} %param.5) | copy-start | bytes 6291460
  17.7 1.6 %copy-start.1 = (bf16[512,16]{0,1:T(8,128)(2,1)S(1)}, bf16[512,16]{0,1:T(8,128)(2,1)}, u32[]{:S(2)}) copy-start(bf16[512,16]{0,1:T(8,128)(2,1)} %param.7) | copy-start | bytes 49156
  17.7 1.6 %copy-start.2 = (s32[16]{0:T(128)S(1)}, s32[16]{0:T(128)}, u32[]{:S(2)}) copy-start(s32[16]{0:T(128)} %param.9) | copy-start | bytes 196
  17.7 1.6 %copy-start.3 = (s32[16]{0:T(128)S(1)}, s32[16]{0:T(128)}, u32[]{:S(2)}) copy-start(s32[16]{0:T(128)} %param.8) | copy-start | bytes 196
  21.0 20.2 %all-to-all-start = ((f32[8,2048,16]{1,2,0:T(8,128)}), f32[8,2048,16]{1,2,0:T(8,128)S(1)}, u32[]{:S(2)}, u32[]{:S(2)}) async-start(f32[8,2048,16]{1,2,0:T(8,128)} %broadcast_in_dim.7), calls=%async_computation.2 | async-start | bytes 2097152 | tf_op jit(solution)/shard_map/all_to_all | solution.py:15
  46.8 20.5 %all-to-all-start.2 = ((f32[32,1,128]{2,1,0:T(1,128)}), f32[32,1,128]{2,1,0:T(1,128)S(1)}, u32[]{:S(2)}, u32[]{:S(2)}) async-start(f32[32,1,128]{2,1,0:T(1,128)} %reshape.21), calls=%async_computation.4 | async-start | bytes 32768 | tf_op jit(solution)/shard_map/all_to_all | solution.py:35
  68.2 17.8 %all-to-all-start.1 = ((f32[32,1,2562]{2,1,0:T(1,128)}), f32[32,1,2562]{2,1,0:T(1,128)S(1)}, u32[]{:S(2)}, u32[]{:S(2)}) async-start(f32[32,1,2562]{2,1,0:T(1,128)} %broadcast_in_dim.8), calls=%async_computation.3 | async-start | bytes 688128 | tf_op jit(solution)/shard_map/all_to_all | solution.py:15
  72.1 36.4 %reduce-scatter.5.cloned.1.call-start = ((), (), s32[]{:S(2)}) async-start(), calls=%async_computation.6 | async-start | bytes 655360 | tf_op jit(solution)/shard_map/reduce_scatter | solution.py:24
Sparse Core Ops, SparseCore 0:
  17.8 59.6 reduce-scatter.2
  80.0 28.4 reduce-scatter.4
where the time goes:
time: 117 us
  waiting for transfers between devices  52.6 us (45%)
  starting transfers between devices  20.2 us (17%)
  matrix products  15.8 us (14%)
  between operations  14.1 us (12%)
  other arithmetic  9.13 us (8%)
  local copies, waits for them, and re-layouts  5.13 us (4%)
    reduce_scatter x2, waiting for transfers between devices, summed_rows(): total = lax.psum_scatter(total, axis, scatter_dimension=0, tiled=True)  26.7 us
    all_to_all x2, waiting for transfers between devices, sent_to_all(): return lax.all_to_all(copies, axis, split_axis=0, concat_axis=0, tiled=True)  16.6 us
    dot_general x2, matrix products, contract(): lax.dot_general(left, right, (((0,), (0,)), ((), ())), preferred_element_...  15.1 us
    all_to_all x1, starting transfers between devices, sum_at_owner(): lax.all_to_all(blocks, axis, split_axis=0, concat_axis=0, tiled=True)  10.6 us
    all_to_all x2, starting transfers between devices, sent_to_all(): return lax.all_to_all(copies, axis, split_axis=0, concat_axis=0, tiled=True)  9.58 us
    all_to_all x1, waiting for transfers between devices, sum_at_owner(): lax.all_to_all(blocks, axis, split_axis=0, concat_axis=0, tiled=True)  9.21 us
    reduce_sum x1, other arithmetic, per_device(): trait_sq = jnp.sum(jnp.square(phenotypes.astype(jnp.float32)), axis=0)  5.11 us
  transfers between devices with their start and end apart: 5, of which 5 were waited for; matrix products, arithmetic and copies ran while one was open for 14% of the time, Pallas kernels for 0%

commit v1 on v0

v1 whole, which is shorter than its diff:
```python
import jax
import jax.numpy as jnp
from jax import lax
from jax.experimental import pallas as pl
from jax.experimental.pallas import tpu as pltpu
from jax.sharding import Mesh
from jax.sharding import PartitionSpec as P


SAMP = ("samp_0", "samp_1")
EPSILON = 1e-06
CUT = 40


def contract(left, right):
    return lax.dot_general(
        left, right, (((0,), (0,)), ((), ())), preferred_element_type=jnp.float32
    )


def shifted(x, axis, by):
    count = lax.axis_size(axis)
    return lax.ppermute(x, axis, [(i, (i + by) % count) for i in range(count)])


def parted(x, axis):
    count, spots = lax.axis_size(axis), lax.axis_size("pos")
    pairs = []
    for i in range(count):
        for p in range(spots):
            to = (i + (1 if p % 2 == 0 else -1)) % count
            pairs.append((i * spots + p, to * spots + p))
    return lax.ppermute(x, (axis, "pos"), pairs)


def swapped(x, axis):
    return lax.all_to_all(x, axis, split_axis=0, concat_axis=0, tiled=True)


def far_product(place, phenotypes, dosages, groups, ranks):
    depth, traits = phenotypes.shape
    width = dosages.shape[1]
    band = traits // groups
    own = band // ranks

    def body(place, p_ref, d_ref, o_ref, f_ref):
        both = contract(p_ref[...], d_ref[...])
        o_ref[...] = both
        for r in range(ranks):
            f_ref[r] = both[r * own : r * own + CUT]

    return pl.pallas_call(
        body,
        grid_spec=pltpu.PrefetchScalarGridSpec(
            num_scalar_prefetch=1,
            grid=(1,),
            in_specs=[
                pl.BlockSpec((depth, band), lambda i, place: (0, lax.rem(place[0] + groups // 2, groups))),
                pl.BlockSpec((depth, width), lambda i, place: (0, 0)),
            ],
            out_specs=[
                pl.BlockSpec((band, width), lambda i, place: (0, 0)),
                pl.BlockSpec((ranks, CUT, width), lambda i, place: (0, 0, 0)),
            ],
        ),
        out_shape=[
            jax.ShapeDtypeStruct((band, width), jnp.float32),
            jax.ShapeDtypeStruct((ranks, CUT, width), jnp.float32),
        ],
        compiler_params=pltpu.CompilerParams(vmem_limit_bytes=56 * 2**20),
        cost_estimate=pl.CostEstimate(
            flops=2 * depth * band * width, bytes_accessed=2 * depth * (band + width), transcendentals=0
        ),
        name="far_product",
    )(place[0], phenotypes, dosages)


def products(far, place, phenotypes, dosages, weights, begin, end, groups, ranks, spots):
    depth, traits = phenotypes.shape
    genes, width = weights.shape
    mine = genes // spots
    band = traits // groups
    own = band // ranks
    rest = own - CUT

    def at(i, place):
        k = jnp.where(i % 2 == 1, groups // 2 - (i + 1) // 2, i // 2 + groups // 2)
        return lax.rem(place[0] + k, groups)

    def body(place, spot, turn, first, last, c_ref, p_ref, d_ref, w_ref, y0_ref, y1_ref, y2_ref, y3_ref, z_ref, t_ref, q_ref, g_ref, held, blocks, low_w, sems):
        i = pl.program_id(0)

        def fetch(step):
            cols = pl.ds(pl.multiple_of(at(step, place) * band, band), band)
            slot = step % 2
            return pltpu.make_async_copy(p_ref.at[:, cols], blocks.at[slot], sems.at[slot])

        @pl.when(i == 0)
        def _():
            fetch(i).start()

        @pl.when(i + 1 < groups)
        def _():
            fetch(i + 1).start()

        @pl.when(i == 0)
        def _():
            d = d_ref[...].astype(jnp.float32)
            q_ref[...] = jnp.sum(d * d, axis=0, keepdims=True)
            gene = lax.broadcasted_iota(jnp.int32, (genes, width), 0)
            position = spot[0] * width + lax.broadcasted_iota(jnp.int32, (genes, width), 1)
            low, high = jnp.zeros_like(gene), jnp.zeros_like(gene)
            for g in range(genes):
                low = jnp.where(gene == g, first[g], low)
                high = jnp.where(gene == g, last[g], high)
            w = w_ref[...].astype(jnp.float32)
            w = jnp.where((position >= low) & (position < high), w, 0.0).astype(jnp.bfloat16)
            value = lax.dot_general(
                w, d_ref[...], (((1,), (1,)), ((), ())), preferred_element_type=jnp.float32
            )
            low_w[...] = w
            for s in range(spots):
                g_ref[s, :mine] = value[s * mine : (s + 1) * mine, :]

        fetch(i).wait()
        here = blocks[i % 2]

        @pl.when(i == 0)
        def _():
            held[...] = c_ref[...]

        @pl.when(i > 0)
        def _():
            held[...] = contract(here, d_ref[...])

        both = held[...]
        upper = both.astype(jnp.bfloat16)
        lower = (both - upper.astype(jnp.float32)).astype(jnp.bfloat16)
        cross = sum(
            lax.dot_general(low_w[...], part, (((1,), (1,)), ((), ())), preferred_element_type=jnp.float32)
            for part in (upper, lower)
        )
        cols = pl.ds(pl.multiple_of(at(i, place) * band, band), band)
        for s in range(spots):
            g_ref[s, mine:, cols] = cross[s * mine : (s + 1) * mine, :]

        @pl.when(pl.program_id(0) > 0)
        def _():
            for r in range(ranks):
                z_ref[0, r] = held[r * own : r * own + CUT, :]

        for k, out in enumerate((y0_ref, y1_ref, y2_ref, y3_ref)):
            start = lax.rem(turn[0] + k, ranks) * own + CUT
            out[0] = held[pl.ds(pl.multiple_of(start, 8), rest), :]
        p = here.astype(jnp.float32)
        t_ref[...] = jnp.sum(p * p, axis=0, keepdims=True)

    whole = lambda i, place, *_: (0, 0)
    piece = jax.ShapeDtypeStruct((groups, rest, width), jnp.float32)
    return pl.pallas_call(
        body,
        grid_spec=pltpu.PrefetchScalarGridSpec(
            num_scalar_prefetch=5,
            grid=(groups,),
            in_specs=[
                pl.BlockSpec((band, width), whole),
                pl.BlockSpec(memory_space=pltpu.HBM),
                pl.BlockSpec((depth, width), whole),
                pl.BlockSpec((genes, width), whole),
            ],
            out_specs=[pl.BlockSpec((1, rest, width), lambda i, place, *_: (at(i, place), 0, 0))] * ranks
            + [
                pl.BlockSpec((1, ranks, CUT, width), lambda i, place, *_: (jnp.maximum(i - 1, 0), 0, 0, 0)),
                pl.BlockSpec((1, band), lambda i, place, *_: (0, at(i, place))),
                pl.BlockSpec((1, width), whole),
                pl.BlockSpec((spots, 2 * mine, depth), lambda i, place, *_: (0, 0, 0)),
            ],
            scratch_shapes=[
                pltpu.VMEM((band, width), jnp.float32),
                pltpu.VMEM((2, depth, band), jnp.bfloat16),
                pltpu.VMEM((genes, width), jnp.bfloat16),
                pltpu.SemaphoreType.DMA((2,)),
            ],
        ),
        out_shape=[piece] * ranks
        + [
            jax.ShapeDtypeStruct((groups - 1, ranks, CUT, width), jnp.float32),
            jax.ShapeDtypeStruct((1, traits), jnp.float32),
            jax.ShapeDtypeStruct((1, width), jnp.float32),
            jax.ShapeDtypeStruct((spots, 2 * mine, depth), jnp.float32),
        ],
        compiler_params=pltpu.CompilerParams(vmem_limit_bytes=56 * 2**20),
        cost_estimate=pl.CostEstimate(
            flops=2 * depth * traits * width, bytes_accessed=2 * depth * (traits + width), transcendentals=0
        ),
        name="products",
    )(place[0], place[2], place[1], begin, end, far, phenotypes, dosages, weights)


def small_sums(parts, trait_sq, dose_sq, groups):
    spots, rows, _ = parts.shape
    mine = rows // 2
    band = trait_sq.shape[1] // groups
    width = dose_sq.shape[1]

    def body(g_ref, t_ref, q_ref, o_ref):
        total = g_ref[0]
        for s in range(1, spots):
            total = total + g_ref[s]
        predicted = total[:mine]
        squares = jnp.sum(predicted * predicted, axis=1, keepdims=True)
        o_ref[...] = jnp.zeros_like(o_ref)
        for g in range(groups):
            cols = slice(g * band, (g + 1) * band)
            o_ref[8 * g : 8 * g + mine, :band] = total[mine:, cols]
            o_ref[8 * g + 2 : 8 * g + 3, :band] = t_ref[:, cols]
            o_ref[8 * g + 3 : 8 * g + 4, :] = q_ref[...]
            o_ref[8 * g + 4 : 8 * g + 4 + mine, :] = jnp.broadcast_to(squares, (mine, width))

    return pl.pallas_call(
        body,
        out_shape=jax.ShapeDtypeStruct((8 * groups, width), jnp.float32),
        compiler_params=pltpu.CompilerParams(vmem_limit_bytes=8 * 2**20),
        cost_estimate=pl.CostEstimate(flops=10**6, bytes_accessed=10**6, transcendentals=0),
        name="small_sums",
    )(parts, trait_sq, dose_sq)


def joined(pieces, extras):
    groups, rest, width = pieces[0].shape
    count = len(pieces)

    def body(*refs):
        o_ref = refs[-1]
        total = refs[0][...]
        for ref in refs[1:count]:
            total = total + ref[...]
        o_ref[:, :rest, :] = total
        small = refs[count][...]
        for ref in refs[count + 1 : -1]:
            small = small + ref[...]
        for g in range(groups):
            o_ref[g, rest:, :] = small[8 * g : 8 * g + 8, :]

    return pl.pallas_call(
        body,
        out_shape=jax.ShapeDtypeStruct((groups, rest + 8, width), jnp.float32),
        compiler_params=pltpu.CompilerParams(vmem_limit_bytes=16 * 2**20),
        cost_estimate=pl.CostEstimate(
            flops=count * pieces[0].size, bytes_accessed=20 * pieces[0].size, transcendentals=0
        ),
        name="joined",
    )(*pieces, *extras)


def device_part(dosages, phenotypes, gene_weights, gene_start, gene_end):
    _, gene_count = gene_weights.shape
    groups, ranks, spots = (lax.axis_size(a) for a in ("samp_0", "samp_1", "pos"))
    z, y, x = (lax.axis_index(a) for a in ("samp_0", "samp_1", "pos"))
    samples = dosages.shape[0] * groups * ranks
    traits = phenotypes.shape[1]
    band = traits // groups
    own = band // ranks
    rest = own - CUT
    mine = gene_count // spots
    forward = lax.rem(x, 2) == 0

    place = (z.reshape(1), y.reshape(1), x.reshape(1))
    far, z_far = far_product(place, phenotypes, dosages, groups, ranks)
    z_in = parted(z_far, "samp_0")
    y0, y1, y2, y3, z_own, trait_sq, dose_sq, partial_value = products(
        far, place, phenotypes, dosages, gene_weights.T, gene_start, gene_end, groups, ranks, spots
    )
    arrived = [shifted(y2, "samp_1", 2), shifted(y1, "samp_1", 1), shifted(y3, "samp_1", -1)]
    parts = swapped(partial_value, "pos")

    nothing = jnp.zeros_like(z_in)
    z_right = shifted(z_own[0] + jnp.where(forward, z_in, nothing), "samp_0", 1)
    z_left = shifted(z_own[1] + jnp.where(forward, nothing, z_in), "samp_0", -1)

    extra = small_sums(parts, trait_sq, dose_sq, groups)
    extras = [extra] + [shifted(extra, "samp_1", k) for k in (2, 1, 3)]

    for at in (2, 4):
        z_right, z_left = lax.optimization_barrier((z_right, z_left))
        z_right = shifted(z_own[at] + z_right, "samp_0", 1)
        z_left = shifted(z_own[at + 1] + z_left, "samp_0", -1)

    second = joined([y0] + arrived, extras)
    second = swapped(second, "samp_0").sum(axis=0)

    first = z_own[6] + z_right + z_left

    def for_rank(k):
        return lax.dynamic_index_in_dim(first, lax.rem(y + k, ranks), 0, False)

    first = for_rank(0) + sum(shifted(for_rank(k), "samp_1", k) for k in (2, 1, 3))

    small = second[rest:]
    mean_dose = small[3] / samples
    mean_pred = small[4 : 4 + mine, 0] / samples
    here = lax.dynamic_slice_in_dim(small[: mine + 1], y * own, own, 1)
    gene_cross = here[:mine].T
    mean_trait = here[mine] / samples
    marginal = jnp.concatenate([first, second[:rest]], 0)
    variant_z = marginal / jnp.sqrt(
        samples * (mean_trait[:, None] + EPSILON) * (mean_dose[None, :] + EPSILON)
    )
    gene_z = gene_cross / jnp.sqrt(
        samples * (mean_trait[:, None] + EPSILON) * (mean_pred[None, :] + EPSILON)
    )
    return (variant_z, gene_z)


def solution(mesh):
    finer = Mesh(mesh.devices.reshape(8, 4, mesh.shape["pos"]), ("samp_0", "samp_1", "pos"))
    in_specs = (P(SAMP, "pos"), P(SAMP, None), P("pos", None), P(), P())
    out_specs = (P(SAMP, "pos"), P(SAMP, "pos"))
    return jax.shard_map(device_part, mesh=finer, in_specs=in_specs, out_specs=out_specs, check_vma=False)
```

time: 117 us -> 115 us (0.983)
  starting transfers between devices: 20.2 us -> 41.7 us
  Pallas kernels: 0 us -> 19.3 us
  matrix products: 15.8 us -> 0 us
  between operations: 14.1 us -> 0.72 us
  waiting for transfers between devices: 52.6 us -> 44.6 us
  local copies, waits for them, and re-layouts: 5.13 us -> 1.5 us
  other arithmetic: 9.13 us -> 6.15 us
    ppermute x0 -> x16, waiting for transfers between devices: none -> 39.7 us  [the longest x15 39.7 us: shifted(): return lax.ppermute(x, axis, [(i, (i + by) % count) for i in range(count)])]
    ppermute x0 -> x16, starting transfers between devices: none -> 30.1 us  [the longest x15 28.9 us: shifted(): return lax.ppermute(x, axis, [(i, (i + by) % count) for i in range(count)])]
    reduce_scatter x2 -> x0, waiting for transfers between devices: 26.7 us -> none  [summed_rows(): total = lax.psum_scatter(total, axis, scatter_dimension=0, tiled=True)]
    all_to_all x3 -> x2, waiting for transfers between devices: 25.8 us -> 4.88 us  [swapped(): return lax.all_to_all(x, axis, split_axis=0, concat_axis=0, tiled=True)]
    pallas_call x0 -> x4, Pallas kernels: none -> 19.3 us  [the longest x1 14.7 us: products(): pl.pallas_call(body, grid_spec=pltpu.PrefetchScalarGridSpec(num_scalar_pr...]
    dot_general x3 -> x0, matrix products: 15.8 us -> none  [the longest x2 15.1 us: contract(): lax.dot_general(left, right, (((0,), (0,)), ((), ())), preferred_element_...]
    all_to_all x3 -> x2, starting transfers between devices: 20.2 us -> 11.6 us  [swapped(): return lax.all_to_all(x, axis, split_axis=0, concat_axis=0, tiled=True)]
    reduce_sum x6 -> x1, other arithmetic: 6.07 us -> 0.04 us  [device_part(): second = swapped(second, 'samp_0').sum(axis=0)]
  transfers between devices with their start and end apart: 5 -> 18, of which waited for: 5 -> 7; matrix products, arithmetic and copies ran while one was open for 14% -> 4% of each run, Pallas kernels for 0% -> 1%
where the time goes in v1:
time: 115 us; the launch traced here: 114 us
  waiting for transfers between devices  44.6 us (39%)
  starting transfers between devices  41.7 us (36%)
  Pallas kernels  19.3 us (17%)
  other arithmetic  6.15 us (5%)
  local copies, waits for them, and re-layouts  1.5 us (1%)
    ppermute x15, waiting for transfers between devices, shifted(): return lax.ppermute(x, axis, [(i, (i + by) % count) for i in range(count)])  39.7 us
    ppermute x15, starting transfers between devices, shifted(): return lax.ppermute(x, axis, [(i, (i + by) % count) for i in range(count)])  28.9 us
    pallas_call x1, Pallas kernels, products(): pl.pallas_call(body, grid_spec=pltpu.PrefetchScalarGridSpec(num_scalar_pr...  14.7 us
    all_to_all x2, starting transfers between devices, swapped(): return lax.all_to_all(x, axis, split_axis=0, concat_axis=0, tiled=True)  11.6 us
    all_to_all x2, waiting for transfers between devices, swapped(): return lax.all_to_all(x, axis, split_axis=0, concat_axis=0, tiled=True)  4.88 us
    pallas_call x1, Pallas kernels, far_product(): pl.pallas_call(body, grid_spec=pltpu.PrefetchScalarGridSpec(num_scalar_pr...  3.61 us
  transfers between devices with their start and end apart: 18, of which 7 were waited for; matrix products, arithmetic and copies ran while one was open for 4% of the time, Pallas kernels for 1%

profile of v1, /device:TPU:2, one launch (start us, length us, event | category | flops | bytes accessed | tf_op | source)
XLA Modules:
  0.0 114.0 jit_solution(8178515197464335500)
XLA Ops:
  0.6 3.6 %far_product.1 = (f32[256,512]{1,0:T(8,128)}, f32[4,40,512]{2,1,0:T(8,128)}) custom-call(s32[1]{0:T(128)} %bitcast.place, bf16[2048,2048]{1,0:T(8,128)(2,1)} %p_ref.3, bf16[2048,512]{1,0:T(8,128)(2,1)} %d_ref.3), custom_call_target="tpu_custom_call" | custom-call | flops 536870912 | bytes 3145728 | tf_op jit(solution)/shard_map/far_product/pallas_call | solution.py:52
  4.3 14.7 %products.1 = (f32[8,24,512]{2,1,0:T(8,128)}, f32[8,24,512]{2,1,0:T(8,128)}, f32[8,24,512]{2,1,0:T(8,128)}, f32[8,24,512]{2,1,0:T(8,128)}, f32[7,4,40,512]{3,2,1...) custom-call(s32[1]{0:T(128)} %bitcast.place, s32[1]{0:T(128)} %bitcast.1.spot, ...), custom_call_target="tpu_custom_call" | custom-call | flops 4294967296 | bytes 10485760 | tf_op jit(solution)/shard_map/products/pallas_call | solution.py:160
  18.9 5.7 %all-to-all-start = ((f32[8,4,2048]{2,1,0:T(4,128)}), f32[8,4,2048]{2,1,0:T(4,128)S(1)}, u32[]{:S(2)}, u32[]{:S(2)}) async-start(f32[8,4,2048]{2,1,0:T(4,128)} %get-tuple-element.27), calls=%async_computation | async-start | bytes 524288 | tf_op jit(solution)/shard_map/all_to_all | solution.py:37
  24.6 1.2 %collective-permute-start = (f32[4,40,512]{2,1,0:T(8,128)S(1)}, f32[4,40,512]{2,1,0:T(8,128)S(1)}, u32[]{:S(2)}, u32[]{:S(2)}) collective-permute-start(f32[4,40,512]{2,1,0:T(8,128)S(1)} %copy-done.3), channel_id=1, source_target_pairs={{0,32},{1,225},{2,34},{3,227},{4,36},{5,229},{6,38},{7,231},{32,64... | collective-permute-start | bytes 983048 | tf_op jit(solution)/shard_map/ppermute | solution.py:33
  25.8 4.9 %all-to-all-done.g_ref = f32[8,4,2048]{2,1,0:T(4,128)S(1)} async-done(((f32[8,4,2048]{2,1,0:T(4,128)}), f32[8,4,2048]{2,1,0:T(4,128)S(1)}, u32[]{:S(2)}, u32[]{:S(2)}) %all-to-all-start) | async-done | bytes 262176 | tf_op jit(solution)/shard_map/all_to_all | solution.py:37
  30.7 0.7 copy-done.1
  31.4 0.7 copy-done.2
  32.2 2.5 %collective-permute-start.13 = (f32[64,512]{1,0:T(8,128)S(1)}, f32[64,512]{1,0:T(8,128)S(1)}, u32[]{:S(2)}, u32[]{:S(2)}) collective-permute-start(f32[64,512]{1,0:T(8,128)S(1)} %small_sums.1.refs_4_), channel_id=1, source_target_pairs={{0,16},{8,24},{16,0},{24,8},{1,17},{9,25},{17,1},{25,9},{2,18},{10... | collective-permute-start | bytes 393224 | tf_op jit(solution)/shard_map/ppermute | solution.py:23
  34.7 1.1 collective-permute-start.10
  35.8 0.8 collective-permute-start.11
  36.6 2.4 %collective-permute-start.12 = (f32[8,24,512]{2,1,0:T(8,128)}, f32[8,24,512]{2,1,0:T(8,128)S(1)}, u32[]{:S(2)}, u32[]{:S(2)}) collective-permute-start(f32[8,24,512]{2,1,0:T(8,128)} %get-tuple-element.26), channel_id=1, source_target_pairs={{0,24},{8,0},{16,8},{24,16},{1,25},{9,1},{17,9},{25,17},{2,26},{10... | collective-permute-start | bytes 1179656 | tf_op jit(solution)/shard_map/ppermute | solution.py:23
  39.1 3.4 %collective-permute-start.15 = (f32[64,512]{1,0:T(8,128)S(1)}, f32[64,512]{1,0:T(8,128)S(1)}, u32[]{:S(2)}, u32[]{:S(2)}) collective-permute-start(f32[64,512]{1,0:T(8,128)S(1)} %small_sums.1.refs_4_), channel_id=1, source_target_pairs={{0,24},{8,0},{16,8},{24,16},{1,25},{9,1},{17,9},{25,17},{2,26},{10... | collective-permute-start | bytes 393224 | tf_op jit(solution)/shard_map/ppermute | solution.py:23
  42.5 1.2 %bitcast_add_fusion.2 = (f32[4,40,512]{2,1,0:T(8,128)S(1)}, f32[4,40,512]{2,1,0:T(8,128)S(1)}) fusion(f32[4,40,512]{2,1,0:T(8,128)S(1)} %collective-permute-done, f32[7,4,40,512]{3,2,1,0:T(8,128)} %get-tuple-element.17, pred[]{:T(512)S(6)} %eq.3), kind=kLoop, calls=%fused_computation.2 | loop fusion | flops 327680 | bytes 1638401 | tf_op jit(solution)/shard_map/add | solution.py:279
  43.7 14.7 %collective-permute-done.14.refs_6_ = f32[64,512]{1,0:T(8,128)S(1)} collective-permute-done((f32[64,512]{1,0:T(8,128)S(1)}, f32[64,512]{1,0:T(8,128)S(1)}, u32[]{:S(2)}, u32[]{:S(2)}) %collective-permute-start.14) | collective-permute-done | bytes 131104 | tf_op jit(solution)/shard_map/ppermute | solution.py:23
  58.4 1.2 %collective-permute-start.1 = (f32[4,40,512]{2,1,0:T(8,128)S(1)}, f32[4,40,512]{2,1,0:T(8,128)S(1)}, u32[]{:S(2)}, u32[]{:S(2)}) collective-permute-start(f32[4,40,512]{2,1,0:T(8,128)S(1)} %get-tuple-element.31), channel_id=1, source_target_pairs={{0,32},{32,64},{64,96},{96,128},{128,160},{160,192},{192,224},{224... | collective-permute-start | bytes 983048 | tf_op jit(solution)/shard_map/ppermute | solution.py:23
  59.6 4.2 %collective-permute-start.2 = (f32[4,40,512]{2,1,0:T(8,128)S(1)}, f32[4,40,512]{2,1,0:T(8,128)S(1)}, u32[]{:S(2)}, u32[]{:S(2)}) collective-permute-start(f32[4,40,512]{2,1,0:T(8,128)S(1)} %get-tuple-element.30), channel_id=1, source_target_pairs={{0,224},{32,0},{64,32},{96,64},{128,96},{160,128},{192,160},{224,1... | collective-permute-start | bytes 983048 | tf_op jit(solution)/shard_map/ppermute | solution.py:23
  63.8 0.9 joined.1
  64.7 5.9 %all-to-all-start.1 = ((f32[8,32,512]{2,1,0:T(8,128)}), f32[8,32,512]{2,1,0:T(8,128)S(1)}, u32[]{:S(2)}, u32[]{:S(2)}) async-start(f32[8,32,512]{2,1,0:T(8,128)} %joined.1), calls=%async_computation.1 | async-start | bytes 1048576 | tf_op jit(solution)/shard_map/all_to_all | solution.py:37
  70.7 0.6 collective-permute-done.1
  71.3 1.2 %bitcast_add_fusion.1 = (f32[4,40,512]{2,1,0:T(8,128)S(1)}, f32[4,40,512]{2,1,0:T(8,128)S(1)}) fusion(f32[4,40,512]{2,1,0:T(8,128)S(1)} %collective-permute-done.2, f32[7,4,40,512]{3,2,1,0:T(8,128)} %get-tuple-element.17, f32[4,40,512]{2,1,0:T(8,128)S(1)} %collective-permute-done.1), kind=kLoop, calls=%fused_computation.1 | loop fusion | flops 163840 | bytes 1966080 | tf_op jit(solution)/shard_map/add | solution.py:287
  72.5 1.5 %collective-permute-start.3 = (f32[4,40,512]{2,1,0:T(8,128)S(1)}, f32[4,40,512]{2,1,0:T(8,128)S(1)}, u32[]{:S(2)}, u32[]{:S(2)}) collective-permute-start(f32[4,40,512]{2,1,0:T(8,128)S(1)} %get-tuple-element.35), channel_id=1, source_target_pairs={{0,32},{32,64},{64,96},{96,128},{128,160},{160,192},{192,224},{224... | collective-permute-start | bytes 983048 | tf_op jit(solution)/shard_map/ppermute | solution.py:23
  74.0 1.9 %collective-permute-start.4 = (f32[4,40,512]{2,1,0:T(8,128)S(1)}, f32[4,40,512]{2,1,0:T(8,128)S(1)}, u32[]{:S(2)}, u32[]{:S(2)}) collective-permute-start(f32[4,40,512]{2,1,0:T(8,128)S(1)} %get-tuple-element.34), channel_id=1, source_target_pairs={{0,224},{32,0},{64,32},{96,64},{128,96},{160,128},{192,160},{224,1... | collective-permute-start | bytes 983048 | tf_op jit(solution)/shard_map/ppermute | solution.py:23
  75.9 16.1 %collective-permute-done.3 = f32[4,40,512]{2,1,0:T(8,128)S(1)} collective-permute-done((f32[4,40,512]{2,1,0:T(8,128)S(1)}, f32[4,40,512]{2,1,0:T(8,128)S(1)}, u32[]{:S(2)}, u32[]{:S(2)}) %collective-permute-start.3) | collective-permute-done | bytes 327712 | tf_op jit(solution)/shard_map/ppermute | solution.py:23
  91.9 1.2 %bitcast_add_fusion.5 = (f32[4,40,512]{2,1,0:T(8,128)S(1)}, f32[4,40,512]{2,1,0:T(8,128)S(1)}) fusion(f32[4,40,512]{2,1,0:T(8,128)S(1)} %collective-permute-done.3, f32[7,4,40,512]{3,2,1,0:T(8,128)} %get-tuple-element.17, f32[4,40,512]{2,1,0:T(8,128)S(1)} %collective-permute-done.4), kind=kLoop, calls=%fused_computation.5 | loop fusion | flops 163840 | bytes 1966080 | tf_op jit(solution)/shard_map/add | solution.py:286
  93.4 3.0 %collective-permute-start.6 = (f32[4,40,512]{2,1,0:T(8,128)S(1)}, f32[4,40,512]{2,1,0:T(8,128)S(1)}, u32[]{:S(2)}, u32[]{:S(2)}) collective-permute-start(f32[4,40,512]{2,1,0:T(8,128)S(1)} %get-tuple-element.33), channel_id=1, source_target_pairs={{0,224},{32,0},{64,32},{96,64},{128,96},{160,128},{192,160},{224,1... | collective-permute-start | bytes 983048 | tf_op jit(solution)/shard_map/ppermute | solution.py:23
  96.7 6.4 %collective-permute-done.5 = f32[4,40,512]{2,1,0:T(8,128)S(1)} collective-permute-done((f32[4,40,512]{2,1,0:T(8,128)S(1)}, f32[4,40,512]{2,1,0:T(8,128)S(1)}, u32[]{:S(2)}, u32[]{:S(2)}) %collective-permute-start.5) | collective-permute-done | bytes 327712 | tf_op jit(solution)/shard_map/ppermute | solution.py:23
  103.1 1.0 fusion
  104.2 3.3 %collective-permute-start.7 = (f32[40,512]{1,0:T(8,128)S(1)}, f32[40,512]{1,0:T(8,128)S(1)}, u32[]{:S(2)}, u32[]{:S(2)}) collective-permute-start(f32[40,512]{1,0:T(8,128)S(1)} %get-tuple-element.38), channel_id=1, source_target_pairs={{0,16},{8,24},{16,0},{24,8},{1,17},{9,25},{17,1},{25,9},{2,18},{10... | collective-permute-start | bytes 245768 | tf_op jit(solution)/shard_map/ppermute | solution.py:23
  107.6 3.2 %collective-permute-start.9 = (f32[40,512]{1,0:T(8,128)S(1)}, f32[40,512]{1,0:T(8,128)S(1)}, u32[]{:S(2)}, u32[]{:S(2)}) collective-permute-start(f32[40,512]{1,0:T(8,128)S(1)} %get-tuple-element.37), channel_id=1, source_target_pairs={{0,24},{8,0},{16,8},{24,16},{1,25},{9,1},{17,9},{25,17},{2,26},{10... | collective-permute-start | bytes 245768 | tf_op jit(solution)/shard_map/ppermute | solution.py:23
  110.8 0.6 bitcast_multiply_fusion
  111.4 1.8 %collective-permute-done.8 = f32[40,512]{1,0:T(8,128)S(1)} collective-permute-done((f32[40,512]{1,0:T(8,128)S(1)}, f32[40,512]{1,0:T(8,128)S(1)}, u32[]{:S(2)}, u32[]{:S(2)}) %collective-permute-start.8) | collective-permute-done | bytes 81952 | tf_op jit(solution)/shard_map/ppermute | solution.py:23
  113.2 0.8 maximum_multiply_fusion
  (31 shorter events, 0.9 us)
Async XLA Ops:
  4.2 20.4 %copy-start.3 = (f32[4,40,512]{2,1,0:T(8,128)S(1)}, f32[4,40,512]{2,1,0:T(8,128)}, u32[]{:S(2)}) copy-start(f32[4,40,512]{2,1,0:T(8,128)} %get-tuple-element.18) | copy-start | bytes 983044
  18.9 44.9 %copy-start = (f32[8,24,512]{2,1,0:T(8,128)S(1)}, f32[8,24,512]{2,1,0:T(8,128)}, u32[]{:S(2)}) copy-start(f32[8,24,512]{2,1,0:T(8,128)} %get-tuple-element.23.refs_0_) | copy-start | bytes 1179652
  18.9 11.8 %all-to-all-start = ((f32[8,4,2048]{2,1,0:T(4,128)}), f32[8,4,2048]{2,1,0:T(4,128)S(1)}, u32[]{:S(2)}, u32[]{:S(2)}) async-start(f32[8,4,2048]{2,1,0:T(4,128)} %get-tuple-element.27), calls=%async_computation | async-start | bytes 524288 | tf_op jit(solution)/shard_map/all_to_all | solution.py:37
  24.6 14.4 %collective-permute-start = (f32[4,40,512]{2,1,0:T(8,128)S(1)}, f32[4,40,512]{2,1,0:T(8,128)S(1)}, u32[]{:S(2)}, u32[]{:S(2)}) collective-permute-start(f32[4,40,512]{2,1,0:T(8,128)S(1)} %copy-done.3), channel_id=1, source_target_pairs={{0,32},{1,225},{2,34},{3,227},{4,36},{5,229},{6,38},{7,231},{32,64... | collective-permute-start | bytes 983048 | tf_op jit(solution)/shard_map/ppermute | solution.py:33
  30.7 0.7 copy-start.1
  31.4 0.7 copy-start.2
  32.2 6.9 %collective-permute-start.13 = (f32[64,512]{1,0:T(8,128)S(1)}, f32[64,512]{1,0:T(8,128)S(1)}, u32[]{:S(2)}, u32[]{:S(2)}) collective-permute-start(f32[64,512]{1,0:T(8,128)S(1)} %small_sums.1.refs_4_), channel_id=1, source_target_pairs={{0,16},{8,24},{16,0},{24,8},{1,17},{9,25},{17,1},{25,9},{2,18},{10... | collective-permute-start | bytes 393224 | tf_op jit(solution)/shard_map/ppermute | solution.py:23
  34.7 29.1 %collective-permute-start.10 = (f32[8,24,512]{2,1,0:T(8,128)}, f32[8,24,512]{2,1,0:T(8,128)S(1)}, u32[]{:S(2)}, u32[]{:S(2)}) collective-permute-start(f32[8,24,512]{2,1,0:T(8,128)} %get-tuple-element.24), channel_id=1, source_target_pairs={{0,16},{8,24},{16,0},{24,8},{1,17},{9,25},{17,1},{25,9},{2,18},{10... | collective-permute-start | bytes 1179656 | tf_op jit(solution)/shard_map/ppermute | solution.py:23
  35.8 28.0 %collective-permute-start.11 = (f32[8,24,512]{2,1,0:T(8,128)}, f32[8,24,512]{2,1,0:T(8,128)S(1)}, u32[]{:S(2)}, u32[]{:S(2)}) collective-permute-start(f32[8,24,512]{2,1,0:T(8,128)} %get-tuple-element.25), channel_id=1, source_target_pairs={{0,8},{8,16},{16,24},{24,0},{1,9},{9,17},{17,25},{25,1},{2,10},{10... | collective-permute-start | bytes 1179656 | tf_op jit(solution)/shard_map/ppermute | solution.py:23
  36.6 27.2 %collective-permute-start.12 = (f32[8,24,512]{2,1,0:T(8,128)}, f32[8,24,512]{2,1,0:T(8,128)S(1)}, u32[]{:S(2)}, u32[]{:S(2)}) collective-permute-start(f32[8,24,512]{2,1,0:T(8,128)} %get-tuple-element.26), channel_id=1, source_target_pairs={{0,24},{8,0},{16,8},{24,16},{1,25},{9,1},{17,9},{25,17},{2,26},{10... | collective-permute-start | bytes 1179656 | tf_op jit(solution)/shard_map/ppermute | solution.py:23
  39.1 19.4 %collective-permute-start.14 = (f32[64,512]{1,0:T(8,128)S(1)}, f32[64,512]{1,0:T(8,128)S(1)}, u32[]{:S(2)}, u32[]{:S(2)}) collective-permute-start(f32[64,512]{1,0:T(8,128)S(1)} %small_sums.1.refs_4_), channel_id=1, source_target_pairs={{0,8},{8,16},{16,24},{24,0},{1,9},{9,17},{17,25},{25,1},{2,10},{10... | collective-permute-start | bytes 393224 | tf_op jit(solution)/shard_map/ppermute | solution.py:23
  39.1 20.5 %collective-permute-start.15 = (f32[64,512]{1,0:T(8,128)S(1)}, f32[64,512]{1,0:T(8,128)S(1)}, u32[]{:S(2)}, u32[]{:S(2)}) collective-permute-start(f32[64,512]{1,0:T(8,128)S(1)} %small_sums.1.refs_4_), channel_id=1, source_target_pairs={{0,24},{8,0},{16,8},{24,16},{1,25},{9,1},{17,9},{25,17},{2,26},{10... | collective-permute-start | bytes 393224 | tf_op jit(solution)/shard_map/ppermute | solution.py:23
  58.4 12.9 %collective-permute-start.1 = (f32[4,40,512]{2,1,0:T(8,128)S(1)}, f32[4,40,512]{2,1,0:T(8,128)S(1)}, u32[]{:S(2)}, u32[]{:S(2)}) collective-permute-start(f32[4,40,512]{2,1,0:T(8,128)S(1)} %get-tuple-element.31), channel_id=1, source_target_pairs={{0,32},{32,64},{64,96},{96,128},{128,160},{160,192},{192,224},{224... | collective-permute-start | bytes 983048 | tf_op jit(solution)/shard_map/ppermute | solution.py:23
  59.6 11.6 %collective-permute-start.2 = (f32[4,40,512]{2,1,0:T(8,128)S(1)}, f32[4,40,512]{2,1,0:T(8,128)S(1)}, u32[]{:S(2)}, u32[]{:S(2)}) collective-permute-start(f32[4,40,512]{2,1,0:T(8,128)S(1)} %get-tuple-element.30), channel_id=1, source_target_pairs={{0,224},{32,0},{64,32},{96,64},{128,96},{160,128},{192,160},{224,1... | collective-permute-start | bytes 983048 | tf_op jit(solution)/shard_map/ppermute | solution.py:23
  64.7 31.7 %all-to-all-start.1 = ((f32[8,32,512]{2,1,0:T(8,128)}), f32[8,32,512]{2,1,0:T(8,128)S(1)}, u32[]{:S(2)}, u32[]{:S(2)}) async-start(f32[8,32,512]{2,1,0:T(8,128)} %joined.1), calls=%async_computation.1 | async-start | bytes 1048576 | tf_op jit(solution)/shard_map/all_to_all | solution.py:37
  72.5 19.5 %collective-permute-start.3 = (f32[4,40,512]{2,1,0:T(8,128)S(1)}, f32[4,40,512]{2,1,0:T(8,128)S(1)}, u32[]{:S(2)}, u32[]{:S(2)}) collective-permute-start(f32[4,40,512]{2,1,0:T(8,128)S(1)} %get-tuple-element.35), channel_id=1, source_target_pairs={{0,32},{32,64},{64,96},{96,128},{128,160},{160,192},{192,224},{224... | collective-permute-start | bytes 983048 | tf_op jit(solution)/shard_map/ppermute | solution.py:23
  74.0 18.0 %collective-permute-start.4 = (f32[4,40,512]{2,1,0:T(8,128)S(1)}, f32[4,40,512]{2,1,0:T(8,128)S(1)}, u32[]{:S(2)}, u32[]{:S(2)}) collective-permute-start(f32[4,40,512]{2,1,0:T(8,128)S(1)} %get-tuple-element.34), channel_id=1, source_target_pairs={{0,224},{32,0},{64,32},{96,64},{128,96},{160,128},{192,160},{224,1... | collective-permute-start | bytes 983048 | tf_op jit(solution)/shard_map/ppermute | solution.py:23
  93.1 10.0 %collective-permute-start.5 = (f32[4,40,512]{2,1,0:T(8,128)S(1)}, f32[4,40,512]{2,1,0:T(8,128)S(1)}, u32[]{:S(2)}, u32[]{:S(2)}) collective-permute-start(f32[4,40,512]{2,1,0:T(8,128)S(1)} %get-tuple-element.32), channel_id=1, source_target_pairs={{0,32},{32,64},{64,96},{96,128},{128,160},{160,192},{192,224},{224... | collective-permute-start | bytes 983048 | tf_op jit(solution)/shard_map/ppermute | solution.py:23
  93.4 9.7 %collective-permute-start.6 = (f32[4,40,512]{2,1,0:T(8,128)S(1)}, f32[4,40,512]{2,1,0:T(8,128)S(1)}, u32[]{:S(2)}, u32[]{:S(2)}) collective-permute-start(f32[4,40,512]{2,1,0:T(8,128)S(1)} %get-tuple-element.33), channel_id=1, source_target_pairs={{0,224},{32,0},{64,32},{96,64},{128,96},{160,128},{192,160},{224,1... | collective-permute-start | bytes 983048 | tf_op jit(solution)/shard_map/ppermute | solution.py:23
  104.2 7.2 %collective-permute-start.7 = (f32[40,512]{1,0:T(8,128)S(1)}, f32[40,512]{1,0:T(8,128)S(1)}, u32[]{:S(2)}, u32[]{:S(2)}) collective-permute-start(f32[40,512]{1,0:T(8,128)S(1)} %get-tuple-element.38), channel_id=1, source_target_pairs={{0,16},{8,24},{16,0},{24,8},{1,17},{9,25},{17,1},{25,9},{2,18},{10... | collective-permute-start | bytes 245768 | tf_op jit(solution)/shard_map/ppermute | solution.py:23
  107.6 5.7 %collective-permute-start.8 = (f32[40,512]{1,0:T(8,128)S(1)}, f32[40,512]{1,0:T(8,128)S(1)}, u32[]{:S(2)}, u32[]{:S(2)}) collective-permute-start(f32[40,512]{1,0:T(8,128)S(1)} %get-tuple-element.36), channel_id=1, source_target_pairs={{0,8},{8,16},{16,24},{24,0},{1,9},{9,17},{17,25},{25,1},{2,10},{10... | collective-permute-start | bytes 245768 | tf_op jit(solution)/shard_map/ppermute | solution.py:23
  107.6 5.7 %collective-permute-start.9 = (f32[40,512]{1,0:T(8,128)S(1)}, f32[40,512]{1,0:T(8,128)S(1)}, u32[]{:S(2)}, u32[]{:S(2)}) collective-permute-start(f32[40,512]{1,0:T(8,128)S(1)} %get-tuple-element.37), channel_id=1, source_target_pairs={{0,24},{8,0},{16,8},{24,16},{1,25},{9,1},{17,9},{25,17},{2,26},{10... | collective-permute-start | bytes 245768 | tf_op jit(solution)/shard_map/ppermute | solution.py:23

commit v2 on v1

--- a/solution.py
+++ b/solution.py
@@ -9,7 +9,7 @@
 
 SAMP = ("samp_0", "samp_1")
 EPSILON = 1e-06
-CUT = 40
+CUT = 48
 
 
 def contract(left, right):
@@ -43,7 +43,9 @@
     band = traits // groups
     own = band // ranks
 
-    def body(place, p_ref, d_ref, o_ref, f_ref):
+    def body(place, p_ref, d_ref, o_ref, f_ref, q_ref):
+        d = d_ref[...].astype(jnp.float32)
+        q_ref[...] = jnp.sum(d * d, axis=0, keepdims=True)
         both = contract(p_ref[...], d_ref[...])
         o_ref[...] = both
         for r in range(ranks):
@@ -61,11 +63,13 @@
             out_specs=[
                 pl.BlockSpec((band, width), lambda i, place: (0, 0)),
                 pl.BlockSpec((ranks, CUT, width), lambda i, place: (0, 0, 0)),
+                pl.BlockSpec((1, width), lambda i, place: (0, 0)),
             ],
         ),
         out_shape=[
             jax.ShapeDtypeStruct((band, width), jnp.float32),
             jax.ShapeDtypeStruct((ranks, CUT, width), jnp.float32),
+            jax.ShapeDtypeStruct((1, width), jnp.float32),
         ],
         compiler_params=pltpu.CompilerParams(vmem_limit_bytes=56 * 2**20),
         cost_estimate=pl.CostEstimate(
@@ -75,38 +79,66 @@
     )(place[0], phenotypes, dosages)
 
 
-def products(far, place, phenotypes, dosages, weights, begin, end, groups, ranks, spots):
+def products(rel, far, earlier, place, phenotypes, dosages, weights, begin, end, groups, ranks, spots):
     depth, traits = phenotypes.shape
     genes, width = weights.shape
     mine = genes // spots
     band = traits // groups
     own = band // ranks
     rest = own - CUT
+    count, copied = len(rel), far is not None
+    kept = count - 1 if copied else count
 
     def at(i, place):
-        k = jnp.where(i % 2 == 1, groups // 2 - (i + 1) // 2, i // 2 + groups // 2)
+        k = sum(jnp.where(i == j, d + groups, 0) for j, d in enumerate(rel))
         return lax.rem(place[0] + k, groups)
 
-    def body(place, spot, turn, first, last, c_ref, p_ref, d_ref, w_ref, y0_ref, y1_ref, y2_ref, y3_ref, z_ref, t_ref, q_ref, g_ref, held, blocks, low_w, sems):
+    def now(i):
+        return jnp.minimum(i, count - 1)
+
+    def before(i):
+        return jnp.maximum(i - 1, 0)
+
+    def body(place, spot, turn, first, last, p_ref, d_ref, w_ref, *refs):
+        if copied:
+            c_ref, refs = refs[0], refs[1:]
+        if earlier is not None:
+            refs = refs[ranks + 2 :]
+        y_refs, (t_ref, g_ref, z_ref, even, odd, low_w) = refs[:ranks], refs[ranks:]
         i = pl.program_id(0)
 
-        def fetch(step):
-            cols = pl.ds(pl.multiple_of(at(step, place) * band, band), band)
-            slot = step % 2
-            return pltpu.make_async_copy(p_ref.at[:, cols], blocks.at[slot], sems.at[slot])
+        def multiply(to):
+            to[...] = contract(p_ref[...], d_ref[...])
+
+        def squares():
+            p = p_ref[...].astype(jnp.float32)
+            t_ref[...] = jnp.sum(p * p, axis=0, keepdims=True)
+
+        def store(held, keep):
+            both = held[...]
+            if keep:
+                for r in range(ranks):
+                    z_ref[0, r] = both[r * own : r * own + CUT, :]
+            for k, out in enumerate(y_refs):
+                start = lax.rem(turn[0] + k, ranks) * own + CUT
+                out[0] = held[pl.ds(pl.multiple_of(start, 8), rest), :]
+            upper = both.astype(jnp.bfloat16)
+            lower = (both - upper.astype(jnp.float32)).astype(jnp.bfloat16)
+            rows = pl.ds(pl.multiple_of(at(before(i), place) * band, band), band)
+            w = low_w[...]
+            value = lax.dot_general(
+                w, d_ref[rows, :], (((1,), (1,)), ((), ())), preferred_element_type=jnp.float32
+            )
+            cross = sum(
+                lax.dot_general(w, part, (((1,), (1,)), ((), ())), preferred_element_type=jnp.float32)
+                for part in (upper, lower)
+            )
+            for s in range(spots):
+                g_ref[s, :mine] = value[s * mine : (s + 1) * mine, :]
+                g_ref[s, mine:] = cross[s * mine : (s + 1) * mine, :]
 
         @pl.when(i == 0)
         def _():
-            fetch(i).start()
-
-        @pl.when(i + 1 < groups)
-        def _():
-            fetch(i + 1).start()
-
-        @pl.when(i == 0)
-        def _():
-            d = d_ref[...].astype(jnp.float32)
-            q_ref[...] = jnp.sum(d * d, axis=0, keepdims=True)
             gene = lax.broadcasted_iota(jnp.int32, (genes, width), 0)
             position = spot[0] * width + lax.broadcasted_iota(jnp.int32, (genes, width), 1)
             low, high = jnp.zeros_like(gene), jnp.zeros_like(gene)
@@ -114,87 +146,85 @@
                 low = jnp.where(gene == g, first[g], low)
                 high = jnp.where(gene == g, last[g], high)
             w = w_ref[...].astype(jnp.float32)
-            w = jnp.where((position >= low) & (position < high), w, 0.0).astype(jnp.bfloat16)
-            value = lax.dot_general(
-                w, d_ref[...], (((1,), (1,)), ((), ())), preferred_element_type=jnp.float32
-            )
-            low_w[...] = w
-            for s in range(spots):
-                g_ref[s, :mine] = value[s * mine : (s + 1) * mine, :]
-
-        fetch(i).wait()
-        here = blocks[i % 2]
-
-        @pl.when(i == 0)
+            low_w[...] = jnp.where((position >= low) & (position < high), w, 0.0).astype(jnp.bfloat16)
+            if copied:
+                even[...] = c_ref[...]
+            else:
+                multiply(even)
+            squares()
+
+        if copied:
+
+            @pl.when(i == 1)
+            def _():
+                multiply(odd)
+                store(even, False)
+                squares()
+
+        @pl.when((i % 2 == 1) & (i < count) & (i >= (3 if copied else 1)))
         def _():
-            held[...] = c_ref[...]
-
-        @pl.when(i > 0)
+            multiply(odd)
+            store(even, True)
+            squares()
+
+        @pl.when((i % 2 == 0) & (i < count) & (i > 0))
         def _():
-            held[...] = contract(here, d_ref[...])
-
-        both = held[...]
-        upper = both.astype(jnp.bfloat16)
-        lower = (both - upper.astype(jnp.float32)).astype(jnp.bfloat16)
-        cross = sum(
-            lax.dot_general(low_w[...], part, (((1,), (1,)), ((), ())), preferred_element_type=jnp.float32)
-            for part in (upper, lower)
-        )
-        cols = pl.ds(pl.multiple_of(at(i, place) * band, band), band)
-        for s in range(spots):
-            g_ref[s, mine:, cols] = cross[s * mine : (s + 1) * mine, :]
-
-        @pl.when(pl.program_id(0) > 0)
+            multiply(even)
+            store(odd, True)
+            squares()
+
+        @pl.when(i == count)
         def _():
-            for r in range(ranks):
-                z_ref[0, r] = held[r * own : r * own + CUT, :]
-
-        for k, out in enumerate((y0_ref, y1_ref, y2_ref, y3_ref)):
-            start = lax.rem(turn[0] + k, ranks) * own + CUT
-            out[0] = held[pl.ds(pl.multiple_of(start, 8), rest), :]
-        p = here.astype(jnp.float32)
-        t_ref[...] = jnp.sum(p * p, axis=0, keepdims=True)
-
-    whole = lambda i, place, *_: (0, 0)
-    piece = jax.ShapeDtypeStruct((groups, rest, width), jnp.float32)
+            store(odd if count % 2 == 0 else even, True)
+
+    whole = lambda i, *_: (0, 0)
+    in_specs = [
+        pl.BlockSpec((depth, band), lambda i, place, *_: (0, at(now(i), place))),
+        pl.BlockSpec((depth, width), whole),
+        pl.BlockSpec((genes, width), whole),
+    ]
+    operands = [place[0], place[2], place[1], begin, end, phenotypes, dosages, weights]
+    aliases = {}
+    if copied:
+        in_specs.append(pl.BlockSpec((band, width), whole))
+        operands.append(far)
+    if earlier is not None:
+        aliases = {len(operands) + k: k for k in range(len(earlier))}
+        in_specs += [pl.BlockSpec(memory_space=pl.ANY)] * len(earlier)
+        operands += earlier
     return pl.pallas_call(
         body,
         grid_spec=pltpu.PrefetchScalarGridSpec(
             num_scalar_prefetch=5,
-            grid=(groups,),
-            in_specs=[
-                pl.BlockSpec((band, width), whole),
-                pl.BlockSpec(memory_space=pltpu.HBM),
-                pl.BlockSpec((depth, width), whole),
-                pl.BlockSpec((genes, width), whole),
-            ],
-            out_specs=[pl.BlockSpec((1, rest, width), lambda i, place, *_: (at(i, place), 0, 0))] * ranks
+            grid=(count + 1,),
+            in_specs=in_specs,
+            out_specs=[pl.BlockSpec((1, rest, width), lambda i, place, *_: (at(before(i), place), 0, 0))] * ranks
             + [
-                pl.BlockSpec((1, ranks, CUT, width), lambda i, place, *_: (jnp.maximum(i - 1, 0), 0, 0, 0)),
-                pl.BlockSpec((1, band), lambda i, place, *_: (0, at(i, place))),
-                pl.BlockSpec((1, width), whole),
-                pl.BlockSpec((spots, 2 * mine, depth), lambda i, place, *_: (0, 0, 0)),
+                pl.BlockSpec((1, band), lambda i, place, *_: (0, at(now(i), place))),
+                pl.BlockSpec((spots, 2 * mine, band), lambda i, place, *_: (0, 0, at(before(i), place))),
+                pl.BlockSpec(
+                    (1, ranks, CUT, width), lambda i, *_: (jnp.clip(i - 1 - count + kept, 0, kept - 1), 0, 0, 0)
+                ),
             ],
             scratch_shapes=[
                 pltpu.VMEM((band, width), jnp.float32),
-                pltpu.VMEM((2, depth, band), jnp.bfloat16),
+                pltpu.VMEM((band, width), jnp.float32),
                 pltpu.VMEM((genes, width), jnp.bfloat16),
-                pltpu.SemaphoreType.DMA((2,)),
             ],
         ),
-        out_shape=[piece] * ranks
+        out_shape=[jax.ShapeDtypeStruct((groups, rest, width), jnp.float32)] * ranks
         + [
-            jax.ShapeDtypeStruct((groups - 1, ranks, CUT, width), jnp.float32),
             jax.ShapeDtypeStruct((1, traits), jnp.float32),
-            jax.ShapeDtypeStruct((1, width), jnp.float32),
             jax.ShapeDtypeStruct((spots, 2 * mine, depth), jnp.float32),
+            jax.ShapeDtypeStruct((kept, ranks, CUT, width), jnp.float32),
         ],
+        input_output_aliases=aliases,
         compiler_params=pltpu.CompilerParams(vmem_limit_bytes=56 * 2**20),
         cost_estimate=pl.CostEstimate(
-            flops=2 * depth * traits * width, bytes_accessed=2 * depth * (traits + width), transcendentals=0
+            flops=2 * depth * band * count * width, bytes_accessed=2 * depth * (traits + width), transcendentals=0
         ),
         name="products",
-    )(place[0], place[2], place[1], begin, end, far, phenotypes, dosages, weights)
+    )(*operands)
 
 
 def small_sums(parts, trait_sq, dose_sq, groups):
@@ -266,11 +296,12 @@
     forward = lax.rem(x, 2) == 0
 
     place = (z.reshape(1), y.reshape(1), x.reshape(1))
-    far, z_far = far_product(place, phenotypes, dosages, groups, ranks)
+    far, z_far, dose_sq = far_product(place, phenotypes, dosages, groups, ranks)
     z_in = parted(z_far, "samp_0")
-    y0, y1, y2, y3, z_own, trait_sq, dose_sq, partial_value = products(
-        far, place, phenotypes, dosages, gene_weights.T, gene_start, gene_end, groups, ranks, spots
-    )
+    rest_of = (place, phenotypes, dosages, gene_weights.T, gene_start, gene_end, groups, ranks, spots)
+    *earlier, z_own = products((3, -3, 2, -2), None, None, *rest_of)
+    *earlier, z_last = products((4, 1, -1, 0), far, earlier, *rest_of)
+    y0, y1, y2, y3, trait_sq, partial_value = earlier
     arrived = [shifted(y2, "samp_1", 2), shifted(y1, "samp_1", 1), shifted(y3, "samp_1", -1)]
     parts = swapped(partial_value, "pos")
 
@@ -281,15 +312,15 @@
     extra = small_sums(parts, trait_sq, dose_sq, groups)
     extras = [extra] + [shifted(extra, "samp_1", k) for k in (2, 1, 3)]
 
-    for at in (2, 4):
+    for mid in (z_own[2:], z_last):
         z_right, z_left = lax.optimization_barrier((z_right, z_left))
-        z_right = shifted(z_own[at] + z_right, "samp_0", 1)
-        z_left = shifted(z_own[at + 1] + z_left, "samp_0", -1)
+        z_right = shifted(mid[0] + z_right, "samp_0", 1)
+        z_left = shifted(mid[1] + z_left, "samp_0", -1)
 
     second = joined([y0] + arrived, extras)
     second = swapped(second, "samp_0").sum(axis=0)
 
-    first = z_own[6] + z_right + z_left
+    first = z_last[2] + z_right + z_left
 
     def for_rank(k):
         return lax.dynamic_index_in_dim(first, lax.rem(y + k, ranks), 0, False)

time: 115 us -> 103 us (0.90)
  waiting for transfers between devices: 44.6 us -> 37.6 us
  starting transfers between devices: 41.7 us -> 38.8 us
  local copies, waits for them, and re-layouts: 1.5 us -> 0.14 us
  Pallas kernels: 19.3 us -> 20.6 us
    ppermute x15, waiting for transfers between devices: 39.7 us -> 27.9 us  [shifted(): return lax.ppermute(x, axis, [(i, (i + by) % count) for i in range(count)])]
    all_to_all x2, waiting for transfers between devices: 4.88 us -> 9.63 us  [swapped(): return lax.all_to_all(x, axis, split_axis=0, concat_axis=0, tiled=True)]
    ppermute x15, starting transfers between devices: 28.9 us -> 24.4 us  [shifted(): return lax.ppermute(x, axis, [(i, (i + by) % count) for i in range(count)])]
    pallas_call x1 -> x2, Pallas kernels: 14.7 us -> 16.1 us  [products(): pl.pallas_call(body, grid_spec=pltpu.PrefetchScalarGridSpec(num_scalar_pr...]
    unnamed x8 -> x10, local copies, waits for them, and re-layouts: 1.39 us -> 0.02 us
  transfers between devices with their start and end apart: 18 -> 18, of which waited for: 7 -> 10; matrix products, arithmetic and copies ran while one was open for 4% -> 4% of each run, Pallas kernels for 1% -> 17%
where the time goes in v2:
time: 103 us
  starting transfers between devices  38.8 us (38%)
  waiting for transfers between devices  37.6 us (37%)
  Pallas kernels  20.6 us (20%)
  other arithmetic  5.06 us (5%)
    ppermute x15, waiting for transfers between devices, shifted(): return lax.ppermute(x, axis, [(i, (i + by) % count) for i in range(count)])  27.9 us
    ppermute x15, starting transfers between devices, shifted(): return lax.ppermute(x, axis, [(i, (i + by) % count) for i in range(count)])  24.4 us
    pallas_call x2, Pallas kernels, products(): pl.pallas_call(body, grid_spec=pltpu.PrefetchScalarGridSpec(num_scalar_pr...  16.1 us
    all_to_all x2, starting transfers between devices, swapped(): return lax.all_to_all(x, axis, split_axis=0, concat_axis=0, tiled=True)  12.5 us
    all_to_all x2, waiting for transfers between devices, swapped(): return lax.all_to_all(x, axis, split_axis=0, concat_axis=0, tiled=True)  9.63 us
    pallas_call x1, Pallas kernels, far_product(): pl.pallas_call(body, grid_spec=pltpu.PrefetchScalarGridSpec(num_scalar_pr...  3.59 us
    add x1, other arithmetic, device_part(): z_left = shifted(mid[1] + z_left, 'samp_0', -1)  2.11 us
  transfers between devices with their start and end apart: 18, of which 10 were waited for; matrix products, arithmetic and copies ran while one was open for 4% of the time, Pallas kernels for 17%

profile of v2, /device:TPU:2, one launch (start us, length us, event | category | flops | bytes accessed | tf_op | source)
XLA Modules:
  0.0 103.0 jit_solution(3113602785136051658)
XLA Ops:
  0.6 3.6 %far_product.1 = (f32[256,512]{1,0:T(8,128)}, f32[4,48,512]{2,1,0:T(8,128)}, f32[1,512]{1,0:T(1,128)}) custom-call(s32[1]{0:T(128)} %bitcast.place, bf16[2048,2048]{1,0:T(8,128)(2,1)} %p_ref.5, bf16[2048,512]{1,0:T(8,128)(2,1)} %d_ref.5), custom_call_target="tpu_custom_call" | custom-call | flops 536870912 | bytes 3145728 | tf_op jit(solution)/shard_map/far_product/pallas_call | solution.py:54
  4.2 1.9 %collective-permute-start = (f32[4,48,512]{2,1,0:T(8,128)}, f32[4,48,512]{2,1,0:T(8,128)S(1)}, u32[]{:S(2)}, u32[]{:S(2)}) collective-permute-start(f32[4,48,512]{2,1,0:T(8,128)} %get-tuple-element.32), channel_id=1, source_target_pairs={{0,32},{1,225},{2,34},{3,227},{4,36},{5,229},{6,38},{7,231},{32,64... | collective-permute-start | bytes 1179656 | tf_op jit(solution)/shard_map/ppermute | solution.py:33
  6.1 8.3 %products.2 = (f32[8,16,512]{2,1,0:T(8,128)}, f32[8,16,512]{2,1,0:T(8,128)}, f32[8,16,512]{2,1,0:T(8,128)}, f32[8,16,512]{2,1,0:T(8,128)}, f32[1,2048]{1,0:T(1,1...) custom-call(s32[1]{0:T(128)} %bitcast.place, s32[1]{0:T(128)} %bitcast.1.spot, s32[1]{0:T(128)} %bitcast.2.turn, ...), custom_call_target="tpu_custom_call" | custom-call | flops 2147483648 | bytes 10485760 | tf_op jit(solution)/shard_map/products/pallas_call | solution.py:195
  14.4 7.8 %products.3 = (f32[8,16,512]{2,1,0:T(8,128)}, f32[8,16,512]{2,1,0:T(8,128)}, f32[8,16,512]{2,1,0:T(8,128)}, f32[8,16,512]{2,1,0:T(8,128)}, f32[1,2048]{1,0:T(1,1...) custom-call(s32[1]{0:T(128)} %bitcast.place, ...), custom_call_target="tpu_custom_call", output_to_operand_aliasing={{0}: (9, {}), {1}: (10, {}), {2}: (11, {}), {3}: (12, {}), ... | custom-call | flops 2147483648 | bytes 10485760 | tf_op jit(solution)/shard_map/products/pallas_call | solution.py:195
  22.3 8.1 %all-to-all-start = ((f32[8,4,2048]{2,1,0:T(4,128)}), f32[8,4,2048]{2,1,0:T(4,128)S(1)}, u32[]{:S(2)}, u32[]{:S(2)}) async-start(f32[8,4,2048]{2,1,0:T(4,128)} %get-tuple-element.41), calls=%async_computation | async-start | bytes 524288 | tf_op jit(solution)/shard_map/all_to_all | solution.py:37
  30.3 3.2 %collective-permute-start.10 = (f32[8,16,512]{2,1,0:T(8,128)}, f32[8,16,512]{2,1,0:T(8,128)S(1)}, u32[]{:S(2)}, u32[]{:S(2)}) collective-permute-start(f32[8,16,512]{2,1,0:T(8,128)} %get-tuple-element.38), channel_id=1, source_target_pairs={{0,16},{8,24},{16,0},{24,8},{1,17},{9,25},{17,1},{25,9},{2,18},{10... | collective-permute-start | bytes 786440 | tf_op jit(solution)/shard_map/ppermute | solution.py:23
  33.5 0.7 collective-permute-start.11
  34.2 2.6 %collective-permute-start.12 = (f32[8,16,512]{2,1,0:T(8,128)}, f32[8,16,512]{2,1,0:T(8,128)S(1)}, u32[]{:S(2)}, u32[]{:S(2)}) collective-permute-start(f32[8,16,512]{2,1,0:T(8,128)} %get-tuple-element.40), channel_id=1, source_target_pairs={{0,24},{8,0},{16,8},{24,16},{1,25},{9,1},{17,9},{25,17},{2,26},{10... | collective-permute-start | bytes 786440 | tf_op jit(solution)/shard_map/ppermute | solution.py:23
  36.8 1.1 %bitcast_add_fusion.2 = (f32[4,48,512]{2,1,0:T(8,128)}, f32[4,48,512]{2,1,0:T(8,128)}) fusion(f32[4,48,512]{2,1,0:T(8,128)S(1)} %collective-permute-done, f32[4,4,48,512]{3,2,1,0:T(8,128)S(1)} %copy-done.3, pred[]{:T(512)S(6)} %eq.3), kind=kLoop, calls=%fused_computation.2 | loop fusion | flops 393216 | bytes 1966081 | tf_op jit(solution)/shard_map/add | solution.py:310
  37.9 1.0 collective-permute-start.2
  38.8 1.1 %collective-permute-start.1 = (f32[4,48,512]{2,1,0:T(8,128)}, f32[4,48,512]{2,1,0:T(8,128)}, u32[]{:S(2)}, u32[]{:S(2)}) collective-permute-start(f32[4,48,512]{2,1,0:T(8,128)} %get-tuple-element.45), channel_id=1, source_target_pairs={{0,32},{32,64},{64,96},{96,128},{128,160},{160,192},{192,224},{224... | collective-permute-start | bytes 1179656 | tf_op jit(solution)/shard_map/ppermute | solution.py:23
  40.0 1.2 %collective-permute-done.10.refs_1_ = f32[8,16,512]{2,1,0:T(8,128)S(1)} collective-permute-done((f32[8,16,512]{2,1,0:T(8,128)}, f32[8,16,512]{2,1,0:T(8,128)S(1)}, u32[]{:S(2)}, u32[]{:S(2)}) %collective-permute-start.10) | collective-permute-done | bytes 262176 | tf_op jit(solution)/shard_map/ppermute | solution.py:23
  41.3 3.0 %collective-permute-start.15 = (f32[64,512]{1,0:T(8,128)S(1)}, f32[64,512]{1,0:T(8,128)S(1)}, u32[]{:S(2)}, u32[]{:S(2)}) collective-permute-start(f32[64,512]{1,0:T(8,128)S(1)} %small_sums.1.refs_4_), channel_id=1, source_target_pairs={{0,24},{8,0},{16,8},{24,16},{1,25},{9,1},{17,9},{25,17},{2,26},{10... | collective-permute-start | bytes 393224 | tf_op jit(solution)/shard_map/ppermute | solution.py:23
  44.3 1.7 %collective-permute-done.11.refs_2_ = f32[8,16,512]{2,1,0:T(8,128)S(1)} collective-permute-done((f32[8,16,512]{2,1,0:T(8,128)}, f32[8,16,512]{2,1,0:T(8,128)S(1)}, u32[]{:S(2)}, u32[]{:S(2)}) %collective-permute-start.11) | collective-permute-done | bytes 262176 | tf_op jit(solution)/shard_map/ppermute | solution.py:23
  46.0 1.7 %collective-permute-start.14 = (f32[64,512]{1,0:T(8,128)S(1)}, f32[64,512]{1,0:T(8,128)S(1)}, u32[]{:S(2)}, u32[]{:S(2)}) collective-permute-start(f32[64,512]{1,0:T(8,128)S(1)} %small_sums.1.refs_4_), channel_id=1, source_target_pairs={{0,8},{8,16},{16,24},{24,0},{1,9},{9,17},{17,25},{25,1},{2,10},{10... | collective-permute-start | bytes 393224 | tf_op jit(solution)/shard_map/ppermute | solution.py:23
  47.7 1.3 %collective-permute-start.13 = (f32[64,512]{1,0:T(8,128)S(1)}, f32[64,512]{1,0:T(8,128)S(1)}, u32[]{:S(2)}, u32[]{:S(2)}) collective-permute-start(f32[64,512]{1,0:T(8,128)S(1)} %small_sums.1.refs_4_), channel_id=1, source_target_pairs={{0,16},{8,24},{16,0},{24,8},{1,17},{9,25},{17,1},{25,9},{2,18},{10... | collective-permute-start | bytes 393224 | tf_op jit(solution)/shard_map/ppermute | solution.py:23
  49.2 6.4 %collective-permute-done.14.refs_6_ = f32[64,512]{1,0:T(8,128)S(1)} collective-permute-done((f32[64,512]{1,0:T(8,128)S(1)}, f32[64,512]{1,0:T(8,128)S(1)}, u32[]{:S(2)}, u32[]{:S(2)}) %collective-permute-start.14) | collective-permute-done | bytes 131104 | tf_op jit(solution)/shard_map/ppermute | solution.py:23
  55.5 0.8 joined.1
  56.4 4.5 %all-to-all-start.1 = ((f32[8,24,512]{2,1,0:T(8,128)}), f32[8,24,512]{2,1,0:T(8,128)S(1)}, u32[]{:S(2)}, u32[]{:S(2)}) async-start(f32[8,24,512]{2,1,0:T(8,128)} %joined.1), calls=%async_computation.1 | async-start | bytes 786432 | tf_op jit(solution)/shard_map/all_to_all | solution.py:37
  60.8 2.1 %bitcast_add_fusion.1 = (f32[4,48,512]{2,1,0:T(8,128)}, f32[4,48,512]{2,1,0:T(8,128)S(1)}) fusion(f32[4,48,512]{2,1,0:T(8,128)} %collective-permute-done.2, f32[4,4,48,512]{3,2,1,0:T(8,128)S(1)} %copy-done.3, f32[4,48,512]{2,1,0:T(8,128)} %collective-permute-done.1), kind=kLoop, calls=%fused_computation.1 | loop fusion | flops 196608 | bytes 2359296 | tf_op jit(solution)/shard_map/add | solution.py:318
  62.9 3.2 %collective-permute-start.4 = (f32[4,48,512]{2,1,0:T(8,128)}, f32[4,48,512]{2,1,0:T(8,128)S(1)}, u32[]{:S(2)}, u32[]{:S(2)}) collective-permute-start(f32[4,48,512]{2,1,0:T(8,128)} %get-tuple-element.46), channel_id=1, source_target_pairs={{0,224},{32,0},{64,32},{96,64},{128,96},{160,128},{192,160},{224,1... | collective-permute-start | bytes 1179656 | tf_op jit(solution)/shard_map/ppermute | solution.py:23
  66.2 9.6 %all-to-all-done.1 = f32[8,24,512]{2,1,0:T(8,128)S(1)} async-done(((f32[8,24,512]{2,1,0:T(8,128)}), f32[8,24,512]{2,1,0:T(8,128)S(1)}, u32[]{:S(2)}, u32[]{:S(2)}) %all-to-all-start.1) | async-done | bytes 393248 | tf_op jit(solution)/shard_map/all_to_all | solution.py:37
  76.0 3.4 %collective-permute-done.4 = f32[4,48,512]{2,1,0:T(8,128)S(1)} collective-permute-done((f32[4,48,512]{2,1,0:T(8,128)}, f32[4,48,512]{2,1,0:T(8,128)S(1)}, u32[]{:S(2)}, u32[]{:S(2)}) %collective-permute-start.4) | collective-permute-done | bytes 393248 | tf_op jit(solution)/shard_map/ppermute | solution.py:23
  79.4 1.2 %collective-permute-done.3 = f32[4,48,512]{2,1,0:T(8,128)S(1)} collective-permute-done((f32[4,48,512]{2,1,0:T(8,128)S(1)}, f32[4,48,512]{2,1,0:T(8,128)S(1)}, u32[]{:S(2)}, u32[]{:S(2)}) %collective-permute-start.3) | collective-permute-done | bytes 393248 | tf_op jit(solution)/shard_map/ppermute | solution.py:23
  80.8 0.3 collective-permute-start.5
  81.2 3.0 %collective-permute-start.6 = (f32[4,48,512]{2,1,0:T(8,128)S(1)}, f32[4,48,512]{2,1,0:T(8,128)S(1)}, u32[]{:S(2)}, u32[]{:S(2)}) collective-permute-start(f32[4,48,512]{2,1,0:T(8,128)S(1)} %get-tuple-element.49), channel_id=1, source_target_pairs={{0,224},{32,0},{64,32},{96,64},{128,96},{160,128},{192,160},{224,1... | collective-permute-start | bytes 1179656 | tf_op jit(solution)/shard_map/ppermute | solution.py:23
  84.2 8.4 %collective-permute-done.5 = f32[4,48,512]{2,1,0:T(8,128)S(1)} collective-permute-done((f32[4,48,512]{2,1,0:T(8,128)S(1)}, f32[4,48,512]{2,1,0:T(8,128)S(1)}, u32[]{:S(2)}, u32[]{:S(2)}) %collective-permute-start.5) | collective-permute-done | bytes 393248 | tf_op jit(solution)/shard_map/ppermute | solution.py:23
  92.8 3.2 %collective-permute-start.9 = (f32[48,512]{1,0:T(8,128)S(1)}, f32[48,512]{1,0:T(8,128)S(1)}, u32[]{:S(2)}, u32[]{:S(2)}) collective-permute-start(f32[48,512]{1,0:T(8,128)S(1)} %get-tuple-element.51), channel_id=1, source_target_pairs={{0,24},{8,0},{16,8},{24,16},{1,25},{9,1},{17,9},{25,17},{2,26},{10... | collective-permute-start | bytes 294920 | tf_op jit(solution)/shard_map/ppermute | solution.py:23
  96.1 0.6 bitcast_multiply_fusion
  96.7 3.0 %collective-permute-done.8 = f32[48,512]{1,0:T(8,128)S(1)} collective-permute-done((f32[48,512]{1,0:T(8,128)S(1)}, f32[48,512]{1,0:T(8,128)S(1)}, u32[]{:S(2)}, u32[]{:S(2)}) %collective-permute-start.8) | collective-permute-done | bytes 98336 | tf_op jit(solution)/shard_map/ppermute | solution.py:23
  99.7 2.5 %collective-permute-done.7 = f32[48,512]{1,0:T(8,128)S(1)} collective-permute-done((f32[48,512]{1,0:T(8,128)S(1)}, f32[48,512]{1,0:T(8,128)S(1)}, u32[]{:S(2)}, u32[]{:S(2)}) %collective-permute-start.7) | collective-permute-done | bytes 98336 | tf_op jit(solution)/shard_map/ppermute | solution.py:23
  102.2 0.7 maximum_multiply_fusion
  (34 shorter events, 0.9 us)
Async XLA Ops:
  4.2 32.5 %collective-permute-start = (f32[4,48,512]{2,1,0:T(8,128)}, f32[4,48,512]{2,1,0:T(8,128)S(1)}, u32[]{:S(2)}, u32[]{:S(2)}) collective-permute-start(f32[4,48,512]{2,1,0:T(8,128)} %get-tuple-element.32), channel_id=1, source_target_pairs={{0,32},{1,225},{2,34},{3,227},{4,36},{5,229},{6,38},{7,231},{32,64... | collective-permute-start | bytes 1179656 | tf_op jit(solution)/shard_map/ppermute | solution.py:33
  14.4 22.3 %copy-start.3 = (f32[4,4,48,512]{3,2,1,0:T(8,128)S(1)}, f32[4,4,48,512]{3,2,1,0:T(8,128)}, u32[]{:S(2)}) copy-start(f32[4,4,48,512]{3,2,1,0:T(8,128)} %get-tuple-element.31) | copy-start | bytes 4718596
  22.2 17.7 %copy-start.1 = (f32[1,2048]{1,0:T(1,128)S(1)}, f32[1,2048]{1,0:T(1,128)}, u32[]{:S(2)}) copy-start(f32[1,2048]{1,0:T(1,128)} %get-tuple-element.42.t_ref) | copy-start | bytes 24580
  22.2 17.7 %copy-start.2 = (f32[1,512]{1,0:T(1,128)S(1)}, f32[1,512]{1,0:T(1,128)}, u32[]{:S(2)}) copy-start(f32[1,512]{1,0:T(1,128)} %get-tuple-element.43.q_ref) | copy-start | bytes 6148
  22.2 33.3 %copy-start = (f32[8,16,512]{2,1,0:T(8,128)S(1)}, f32[8,16,512]{2,1,0:T(8,128)}, u32[]{:S(2)}) copy-start(f32[8,16,512]{2,1,0:T(8,128)} %get-tuple-element.37.refs_0_) | copy-start | bytes 786436
  22.3 17.6 %all-to-all-start = ((f32[8,4,2048]{2,1,0:T(4,128)}), f32[8,4,2048]{2,1,0:T(4,128)S(1)}, u32[]{:S(2)}, u32[]{:S(2)}) async-start(f32[8,4,2048]{2,1,0:T(4,128)} %get-tuple-element.41), calls=%async_computation | async-start | bytes 524288 | tf_op jit(solution)/shard_map/all_to_all | solution.py:37
  30.3 10.9 %collective-permute-start.10 = (f32[8,16,512]{2,1,0:T(8,128)}, f32[8,16,512]{2,1,0:T(8,128)S(1)}, u32[]{:S(2)}, u32[]{:S(2)}) collective-permute-start(f32[8,16,512]{2,1,0:T(8,128)} %get-tuple-element.38), channel_id=1, source_target_pairs={{0,16},{8,24},{16,0},{24,8},{1,17},{9,25},{17,1},{25,9},{2,18},{10... | collective-permute-start | bytes 786440 | tf_op jit(solution)/shard_map/ppermute | solution.py:23
  33.5 12.5 %collective-permute-start.11 = (f32[8,16,512]{2,1,0:T(8,128)}, f32[8,16,512]{2,1,0:T(8,128)S(1)}, u32[]{:S(2)}, u32[]{:S(2)}) collective-permute-start(f32[8,16,512]{2,1,0:T(8,128)} %get-tuple-element.39), channel_id=1, source_target_pairs={{0,8},{8,16},{16,24},{24,0},{1,9},{9,17},{17,25},{25,1},{2,10},{10... | collective-permute-start | bytes 786440 | tf_op jit(solution)/shard_map/ppermute | solution.py:23
  34.2 13.5 %collective-permute-start.12 = (f32[8,16,512]{2,1,0:T(8,128)}, f32[8,16,512]{2,1,0:T(8,128)S(1)}, u32[]{:S(2)}, u32[]{:S(2)}) collective-permute-start(f32[8,16,512]{2,1,0:T(8,128)} %get-tuple-element.40), channel_id=1, source_target_pairs={{0,24},{8,0},{16,8},{24,16},{1,25},{9,1},{17,9},{25,17},{2,26},{10... | collective-permute-start | bytes 786440 | tf_op jit(solution)/shard_map/ppermute | solution.py:23
  37.9 23.0 %collective-permute-start.2 = (f32[4,48,512]{2,1,0:T(8,128)}, f32[4,48,512]{2,1,0:T(8,128)}, u32[]{:S(2)}, u32[]{:S(2)}) collective-permute-start(f32[4,48,512]{2,1,0:T(8,128)} %get-tuple-element.44), channel_id=1, source_target_pairs={{0,224},{32,0},{64,32},{96,64},{128,96},{160,128},{192,160},{224,1... | collective-permute-start | bytes 1179656 | tf_op jit(solution)/shard_map/ppermute | solution.py:23
  38.8 22.0 %collective-permute-start.1 = (f32[4,48,512]{2,1,0:T(8,128)}, f32[4,48,512]{2,1,0:T(8,128)}, u32[]{:S(2)}, u32[]{:S(2)}) collective-permute-start(f32[4,48,512]{2,1,0:T(8,128)} %get-tuple-element.45), channel_id=1, source_target_pairs={{0,32},{32,64},{64,96},{96,128},{128,160},{160,192},{192,224},{224... | collective-permute-start | bytes 1179656 | tf_op jit(solution)/shard_map/ppermute | solution.py:23
  41.3 7.9 %collective-permute-start.15 = (f32[64,512]{1,0:T(8,128)S(1)}, f32[64,512]{1,0:T(8,128)S(1)}, u32[]{:S(2)}, u32[]{:S(2)}) collective-permute-start(f32[64,512]{1,0:T(8,128)S(1)} %small_sums.1.refs_4_), channel_id=1, source_target_pairs={{0,24},{8,0},{16,8},{24,16},{1,25},{9,1},{17,9},{25,17},{2,26},{10... | collective-permute-start | bytes 393224 | tf_op jit(solution)/shard_map/ppermute | solution.py:23
  46.0 9.5 %collective-permute-start.14 = (f32[64,512]{1,0:T(8,128)S(1)}, f32[64,512]{1,0:T(8,128)S(1)}, u32[]{:S(2)}, u32[]{:S(2)}) collective-permute-start(f32[64,512]{1,0:T(8,128)S(1)} %small_sums.1.refs_4_), channel_id=1, source_target_pairs={{0,8},{8,16},{16,24},{24,0},{1,9},{9,17},{17,25},{25,1},{2,10},{10... | collective-permute-start | bytes 393224 | tf_op jit(solution)/shard_map/ppermute | solution.py:23
  47.7 7.8 %collective-permute-start.13 = (f32[64,512]{1,0:T(8,128)S(1)}, f32[64,512]{1,0:T(8,128)S(1)}, u32[]{:S(2)}, u32[]{:S(2)}) collective-permute-start(f32[64,512]{1,0:T(8,128)S(1)} %small_sums.1.refs_4_), channel_id=1, source_target_pairs={{0,16},{8,24},{16,0},{24,8},{1,17},{9,25},{17,1},{25,9},{2,18},{10... | collective-permute-start | bytes 393224 | tf_op jit(solution)/shard_map/ppermute | solution.py:23
  56.4 19.4 %all-to-all-start.1 = ((f32[8,24,512]{2,1,0:T(8,128)}), f32[8,24,512]{2,1,0:T(8,128)S(1)}, u32[]{:S(2)}, u32[]{:S(2)}) async-start(f32[8,24,512]{2,1,0:T(8,128)} %joined.1), calls=%async_computation.1 | async-start | bytes 786432 | tf_op jit(solution)/shard_map/all_to_all | solution.py:37
  60.8 19.9 %copy-start.4 = (f32[3,4,48,512]{3,2,1,0:T(8,128)S(1)}, f32[3,4,48,512]{3,2,1,0:T(8,128)}, u32[]{:S(2)}) copy-start(f32[3,4,48,512]{3,2,1,0:T(8,128)} %get-tuple-element.30) | copy-start | bytes 3538948
  62.9 16.5 %collective-permute-start.4 = (f32[4,48,512]{2,1,0:T(8,128)}, f32[4,48,512]{2,1,0:T(8,128)S(1)}, u32[]{:S(2)}, u32[]{:S(2)}) collective-permute-start(f32[4,48,512]{2,1,0:T(8,128)} %get-tuple-element.46), channel_id=1, source_target_pairs={{0,224},{32,0},{64,32},{96,64},{128,96},{160,128},{192,160},{224,1... | collective-permute-start | bytes 1179656 | tf_op jit(solution)/shard_map/ppermute | solution.py:23
  66.2 14.5 %collective-permute-start.3 = (f32[4,48,512]{2,1,0:T(8,128)S(1)}, f32[4,48,512]{2,1,0:T(8,128)S(1)}, u32[]{:S(2)}, u32[]{:S(2)}) collective-permute-start(f32[4,48,512]{2,1,0:T(8,128)S(1)} %get-tuple-element.47), channel_id=1, source_target_pairs={{0,32},{32,64},{64,96},{96,128},{128,160},{160,192},{192,224},{224... | collective-permute-start | bytes 1179656 | tf_op jit(solution)/shard_map/ppermute | solution.py:23
  80.8 11.7 %collective-permute-start.5 = (f32[4,48,512]{2,1,0:T(8,128)S(1)}, f32[4,48,512]{2,1,0:T(8,128)S(1)}, u32[]{:S(2)}, u32[]{:S(2)}) collective-permute-start(f32[4,48,512]{2,1,0:T(8,128)S(1)} %get-tuple-element.48), channel_id=1, source_target_pairs={{0,32},{32,64},{64,96},{96,128},{128,160},{160,192},{192,224},{224... | collective-permute-start | bytes 1179656 | tf_op jit(solution)/shard_map/ppermute | solution.py:23
  81.2 11.4 %collective-permute-start.6 = (f32[4,48,512]{2,1,0:T(8,128)S(1)}, f32[4,48,512]{2,1,0:T(8,128)S(1)}, u32[]{:S(2)}, u32[]{:S(2)}) collective-permute-start(f32[4,48,512]{2,1,0:T(8,128)S(1)} %get-tuple-element.49), channel_id=1, source_target_pairs={{0,224},{32,0},{64,32},{96,64},{128,96},{160,128},{192,160},{224,1... | collective-permute-start | bytes 1179656 | tf_op jit(solution)/shard_map/ppermute | solution.py:23
  92.7 7.0 %collective-permute-start.8 = (f32[48,512]{1,0:T(8,128)S(1)}, f32[48,512]{1,0:T(8,128)S(1)}, u32[]{:S(2)}, u32[]{:S(2)}) collective-permute-start(f32[48,512]{1,0:T(8,128)S(1)} %get-tuple-element.50), channel_id=1, source_target_pairs={{0,8},{8,16},{16,24},{24,0},{1,9},{9,17},{17,25},{25,1},{2,10},{10... | collective-permute-start | bytes 294920 | tf_op jit(solution)/shard_map/ppermute | solution.py:23
  92.8 6.9 %collective-permute-start.9 = (f32[48,512]{1,0:T(8,128)S(1)}, f32[48,512]{1,0:T(8,128)S(1)}, u32[]{:S(2)}, u32[]{:S(2)}) collective-permute-start(f32[48,512]{1,0:T(8,128)S(1)} %get-tuple-element.51), channel_id=1, source_target_pairs={{0,24},{8,0},{16,8},{24,16},{1,25},{9,1},{17,9},{25,17},{2,26},{10... | collective-permute-start | bytes 294920 | tf_op jit(solution)/shard_map/ppermute | solution.py:23
  96.0 6.1 %collective-permute-start.7 = (f32[48,512]{1,0:T(8,128)S(1)}, f32[48,512]{1,0:T(8,128)S(1)}, u32[]{:S(2)}, u32[]{:S(2)}) collective-permute-start(f32[48,512]{1,0:T(8,128)S(1)} %get-tuple-element.52), channel_id=1, source_target_pairs={{0,16},{8,24},{16,0},{24,8},{1,17},{9,25},{17,1},{25,9},{2,18},{10... | collective-permute-start | bytes 294920 | tf_op jit(solution)/shard_map/ppermute | solution.py:23

commit v3 on v2

--- a/solution.py
+++ b/solution.py
@@ -9,7 +9,7 @@
 
 SAMP = ("samp_0", "samp_1")
 EPSILON = 1e-06
-CUT = 48
+CUT = 56
 
 
 def contract(left, right):
@@ -318,7 +318,8 @@
         z_left = shifted(mid[1] + z_left, "samp_0", -1)
 
     second = joined([y0] + arrived, extras)
-    second = swapped(second, "samp_0").sum(axis=0)
+    second = swapped(second, "samp_0")
+    second = second.sum(axis=0)
 
     first = z_last[2] + z_right + z_left
 

time: 103 us -> 102 us (level); the launches traced: 103 us -> 101 us
  waiting for transfers between devices: 37.6 us -> 35.1 us
  starting transfers between devices: 38.8 us -> 36.4 us
  local copies, waits for them, and re-layouts: 0.14 us -> 1.73 us
  other arithmetic: 5.06 us -> 6.39 us
    all_to_all x2, waiting for transfers between devices: 9.63 us -> 6.17 us  [swapped(): return lax.all_to_all(x, axis, split_axis=0, concat_axis=0, tiled=True)]
    ppermute x1, waiting for transfers between devices: 0.01 us -> 2.39 us  [parted(): return lax.ppermute(x, (axis, 'pos'), pairs)]
    all_to_all x2, starting transfers between devices: 12.5 us -> 10.9 us  [swapped(): return lax.all_to_all(x, axis, split_axis=0, concat_axis=0, tiled=True)]
    unnamed x10, local copies, waits for them, and re-layouts: 0.02 us -> 1.61 us
    ppermute x15, waiting for transfers between devices: 27.9 us -> 26.5 us  [shifted(): return lax.ppermute(x, axis, [(i, (i + by) % count) for i in range(count)])]
    add x1, other arithmetic: 1.11 us -> 2.25 us  [device_part(): z_left = shifted(z_own[1] + jnp.where(forward, nothing, z_in), 'samp_0', -1)]
  transfers between devices with their start and end apart: 18 -> 18, of which waited for: 10 -> 11; matrix products, arithmetic and copies ran while one was open for 4% -> 3% of each run, Pallas kernels for 17% -> 17%
where the time goes in v3:
time: 102 us; the launch traced here: 101 us
  starting transfers between devices  36.4 us (36%)
  waiting for transfers between devices  35.1 us (34%)
  Pallas kernels  20.5 us (20%)
  other arithmetic  6.39 us (6%)
  local copies, waits for them, and re-layouts  1.73 us (2%)
    ppermute x15, waiting for transfers between devices, shifted(): return lax.ppermute(x, axis, [(i, (i + by) % count) for i in range(count)])  26.5 us
    ppermute x15, starting transfers between devices, shifted(): return lax.ppermute(x, axis, [(i, (i + by) % count) for i in range(count)])  23.6 us
    pallas_call x2, Pallas kernels, products(): pl.pallas_call(body, grid_spec=pltpu.PrefetchScalarGridSpec(num_scalar_pr...  16 us
    all_to_all x2, starting transfers between devices, swapped(): return lax.all_to_all(x, axis, split_axis=0, concat_axis=0, tiled=True)  10.9 us
    all_to_all x2, waiting for transfers between devices, swapped(): return lax.all_to_all(x, axis, split_axis=0, concat_axis=0, tiled=True)  6.17 us
    pallas_call x1, Pallas kernels, far_product(): pl.pallas_call(body, grid_spec=pltpu.PrefetchScalarGridSpec(num_scalar_pr...  3.66 us
    ppermute x1, waiting for transfers between devices, parted(): return lax.ppermute(x, (axis, 'pos'), pairs)  2.39 us
    add x1, other arithmetic, device_part(): z_left = shifted(mid[1] + z_left, 'samp_0', -1)  2.27 us
  transfers between devices with their start and end apart: 18, of which 11 were waited for; matrix products, arithmetic and copies ran while one was open for 3% of the time, Pallas kernels for 17%

profile of v3, /device:TPU:2, one launch (start us, length us, event | category | flops | bytes accessed | tf_op | source)
XLA Modules:
  0.0 100.9 jit_solution(5421719009535154262)
XLA Ops:
  0.6 3.7 %far_product.1 = (f32[256,512]{1,0:T(8,128)}, f32[4,56,512]{2,1,0:T(8,128)}, f32[1,512]{1,0:T(1,128)}) custom-call(s32[1]{0:T(128)} %bitcast.place, bf16[2048,2048]{1,0:T(8,128)(2,1)} %p_ref.5, bf16[2048,512]{1,0:T(8,128)(2,1)} %d_ref.5), custom_call_target="tpu_custom_call" | custom-call | flops 536870912 | bytes 3145728 | tf_op jit(solution)/shard_map/far_product/pallas_call | solution.py:54
  4.3 1.9 %collective-permute-start = (f32[4,56,512]{2,1,0:T(8,128)}, f32[4,56,512]{2,1,0:T(8,128)S(1)}, u32[]{:S(2)}, u32[]{:S(2)}) collective-permute-start(f32[4,56,512]{2,1,0:T(8,128)} %get-tuple-element.32), channel_id=1, source_target_pairs={{0,32},{1,225},{2,34},{3,227},{4,36},{5,229},{6,38},{7,231},{32,64... | collective-permute-start | bytes 1376264 | tf_op jit(solution)/shard_map/ppermute | solution.py:33
  6.2 8.2 %products.2 = (f32[8,8,512]{2,1,0:T(8,128)}, f32[8,8,512]{2,1,0:T(8,128)}, f32[8,8,512]{2,1,0:T(8,128)}, f32[8,8,512]{2,1,0:T(8,128)}, f32[1,2048]{1,0:T(1,128)}...) custom-call(s32[1]{0:T(128)} %bitcast.place, s32[1]{0:T(128)} %bitcast.1.spot, s32[1]{0:T(128)} %bitcast.2.turn, ...), custom_call_target="tpu_custom_call" | custom-call | flops 2147483648 | bytes 10485760 | tf_op jit(solution)/shard_map/products/pallas_call | solution.py:195
  14.4 2.4 %collective-permute-done = f32[4,56,512]{2,1,0:T(8,128)S(1)} collective-permute-done((f32[4,56,512]{2,1,0:T(8,128)}, f32[4,56,512]{2,1,0:T(8,128)S(1)}, u32[]{:S(2)}, u32[]{:S(2)}) %collective-permute-start) | collective-permute-done | bytes 458784 | tf_op jit(solution)/shard_map/ppermute | solution.py:33
  16.8 2.3 %bitcast_add_fusion.2 = (f32[4,56,512]{2,1,0:T(8,128)}, f32[4,56,512]{2,1,0:T(8,128)}) fusion(f32[4,56,512]{2,1,0:T(8,128)S(1)} %collective-permute-done, f32[4,4,56,512]{3,2,1,0:T(8,128)} %get-tuple-element.31, pred[]{:T(512)S(6)} %eq.3), kind=kLoop, calls=%fused_computation.2 | loop fusion | flops 458752 | bytes 2293761 | tf_op jit(solution)/shard_map/add | solution.py:310
  19.1 2.0 %collective-permute-start.2 = (f32[4,56,512]{2,1,0:T(8,128)}, f32[4,56,512]{2,1,0:T(8,128)}, u32[]{:S(2)}, u32[]{:S(2)}) collective-permute-start(f32[4,56,512]{2,1,0:T(8,128)} %get-tuple-element.44), channel_id=1, source_target_pairs={{0,224},{32,0},{64,32},{96,64},{128,96},{160,128},{192,160},{224,1... | collective-permute-start | bytes 1376264 | tf_op jit(solution)/shard_map/ppermute | solution.py:23
  21.1 7.8 %products.3 = (f32[8,8,512]{2,1,0:T(8,128)}, f32[8,8,512]{2,1,0:T(8,128)}, f32[8,8,512]{2,1,0:T(8,128)}, f32[8,8,512]{2,1,0:T(8,128)}, f32[1,2048]{1,0:T(1,128)}...) custom-call(s32[1]{0:T(128)} %bitcast.place, ...), custom_call_target="tpu_custom_call", output_to_operand_aliasing={{0}: (9, {}), {1}: (10, {}), {2}: (11, {}), {3}: (12, {}), ... | custom-call | flops 2147483648 | bytes 10485760 | tf_op jit(solution)/shard_map/products/pallas_call | solution.py:195
  28.9 5.0 %all-to-all-start = ((f32[8,4,2048]{2,1,0:T(4,128)}), f32[8,4,2048]{2,1,0:T(4,128)S(1)}, u32[]{:S(2)}, u32[]{:S(2)}) async-start(f32[8,4,2048]{2,1,0:T(4,128)} %get-tuple-element.41), calls=%async_computation | async-start | bytes 524288 | tf_op jit(solution)/shard_map/all_to_all | solution.py:37
  33.9 3.2 %collective-permute-start.10 = (f32[8,8,512]{2,1,0:T(8,128)}, f32[8,8,512]{2,1,0:T(8,128)S(1)}, u32[]{:S(2)}, u32[]{:S(2)}) collective-permute-start(f32[8,8,512]{2,1,0:T(8,128)} %get-tuple-element.38), channel_id=1, source_target_pairs={{0,16},{8,24},{16,0},{24,8},{1,17},{9,25},{17,1},{25,9},{2,18},{10... | collective-permute-start | bytes 393224 | tf_op jit(solution)/shard_map/ppermute | solution.py:23
  37.1 0.7 collective-permute-start.11
  37.8 2.6 %collective-permute-start.12 = (f32[8,8,512]{2,1,0:T(8,128)}, f32[8,8,512]{2,1,0:T(8,128)S(1)}, u32[]{:S(2)}, u32[]{:S(2)}) collective-permute-start(f32[8,8,512]{2,1,0:T(8,128)} %get-tuple-element.40), channel_id=1, source_target_pairs={{0,24},{8,0},{16,8},{24,16},{1,25},{9,1},{17,9},{25,17},{2,26},{10... | collective-permute-start | bytes 393224 | tf_op jit(solution)/shard_map/ppermute | solution.py:23
  40.3 0.7 copy-done.1
  41.1 0.8 collective-permute-done.10.refs_1_
  42.0 3.0 %collective-permute-start.15 = (f32[64,512]{1,0:T(8,128)S(1)}, f32[64,512]{1,0:T(8,128)S(1)}, u32[]{:S(2)}, u32[]{:S(2)}) collective-permute-start(f32[64,512]{1,0:T(8,128)S(1)} %small_sums.1.refs_4_), channel_id=1, source_target_pairs={{0,24},{8,0},{16,8},{24,16},{1,25},{9,1},{17,9},{25,17},{2,26},{10... | collective-permute-start | bytes 393224 | tf_op jit(solution)/shard_map/ppermute | solution.py:23
  45.0 0.7 collective-permute-start.14
  45.7 1.6 %collective-permute-start.13 = (f32[64,512]{1,0:T(8,128)S(1)}, f32[64,512]{1,0:T(8,128)S(1)}, u32[]{:S(2)}, u32[]{:S(2)}) collective-permute-start(f32[64,512]{1,0:T(8,128)S(1)} %small_sums.1.refs_4_), channel_id=1, source_target_pairs={{0,16},{8,24},{16,0},{24,8},{1,17},{9,25},{17,1},{25,9},{2,18},{10... | collective-permute-start | bytes 393224 | tf_op jit(solution)/shard_map/ppermute | solution.py:23
  47.3 1.7 %collective-permute-done.15.refs_7_ = f32[64,512]{1,0:T(8,128)S(1)} collective-permute-done((f32[64,512]{1,0:T(8,128)S(1)}, f32[64,512]{1,0:T(8,128)S(1)}, u32[]{:S(2)}, u32[]{:S(2)}) %collective-permute-start.15) | collective-permute-done | bytes 131104 | tf_op jit(solution)/shard_map/ppermute | solution.py:23
  48.9 4.5 %collective-permute-done.14.refs_6_ = f32[64,512]{1,0:T(8,128)S(1)} collective-permute-done((f32[64,512]{1,0:T(8,128)S(1)}, f32[64,512]{1,0:T(8,128)S(1)}, u32[]{:S(2)}, u32[]{:S(2)}) %collective-permute-start.14) | collective-permute-done | bytes 131104 | tf_op jit(solution)/shard_map/ppermute | solution.py:23
  53.5 0.9 copy-done
  54.4 0.8 joined.1
  55.1 5.9 %all-to-all-start.1 = ((f32[8,16,512]{2,1,0:T(8,128)}), f32[8,16,512]{2,1,0:T(8,128)S(1)}, u32[]{:S(2)}, u32[]{:S(2)}) async-start(f32[8,16,512]{2,1,0:T(8,128)} %joined.1), calls=%async_computation.1 | async-start | bytes 524288 | tf_op jit(solution)/shard_map/all_to_all | solution.py:37
  61.1 2.3 %bitcast_add_fusion.1 = (f32[4,56,512]{2,1,0:T(8,128)}, f32[4,56,512]{2,1,0:T(8,128)}) fusion(f32[4,56,512]{2,1,0:T(8,128)} %collective-permute-done.2, f32[4,4,56,512]{3,2,1,0:T(8,128)S(1)} %copy-done.3, f32[4,56,512]{2,1,0:T(8,128)} %collective-permute-done.1), kind=kLoop, calls=%fused_computation.1 | loop fusion | flops 229376 | bytes 2752512 | tf_op jit(solution)/shard_map/add | solution.py:318
  63.3 3.2 %collective-permute-start.4 = (f32[4,56,512]{2,1,0:T(8,128)}, f32[4,56,512]{2,1,0:T(8,128)S(1)}, u32[]{:S(2)}, u32[]{:S(2)}) collective-permute-start(f32[4,56,512]{2,1,0:T(8,128)} %get-tuple-element.46), channel_id=1, source_target_pairs={{0,224},{32,0},{64,32},{96,64},{128,96},{160,128},{192,160},{224,1... | collective-permute-start | bytes 1376264 | tf_op jit(solution)/shard_map/ppermute | solution.py:23
  66.6 6.2 %all-to-all-done.1 = f32[8,16,512]{2,1,0:T(8,128)S(1)} async-done(((f32[8,16,512]{2,1,0:T(8,128)}), f32[8,16,512]{2,1,0:T(8,128)S(1)}, u32[]{:S(2)}, u32[]{:S(2)}) %all-to-all-start.1) | async-done | bytes 262176 | tf_op jit(solution)/shard_map/all_to_all | solution.py:37
  72.9 4.2 %collective-permute-done.4 = f32[4,56,512]{2,1,0:T(8,128)S(1)} collective-permute-done((f32[4,56,512]{2,1,0:T(8,128)}, f32[4,56,512]{2,1,0:T(8,128)S(1)}, u32[]{:S(2)}, u32[]{:S(2)}) %collective-permute-start.4) | collective-permute-done | bytes 458784 | tf_op jit(solution)/shard_map/ppermute | solution.py:23
  77.1 1.9 %collective-permute-done.3 = f32[4,56,512]{2,1,0:T(8,128)S(1)} collective-permute-done((f32[4,56,512]{2,1,0:T(8,128)}, f32[4,56,512]{2,1,0:T(8,128)S(1)}, u32[]{:S(2)}, u32[]{:S(2)}) %collective-permute-start.3) | collective-permute-done | bytes 458784 | tf_op jit(solution)/shard_map/ppermute | solution.py:23
  79.3 3.2 %collective-permute-start.6 = (f32[4,56,512]{2,1,0:T(8,128)S(1)}, f32[4,56,512]{2,1,0:T(8,128)S(1)}, u32[]{:S(2)}, u32[]{:S(2)}) collective-permute-start(f32[4,56,512]{2,1,0:T(8,128)S(1)} %get-tuple-element.49), channel_id=1, source_target_pairs={{0,224},{32,0},{64,32},{96,64},{128,96},{160,128},{192,160},{224,1... | collective-permute-start | bytes 1376264 | tf_op jit(solution)/shard_map/ppermute | solution.py:23
  82.6 7.7 %collective-permute-done.5 = f32[4,56,512]{2,1,0:T(8,128)S(1)} collective-permute-done((f32[4,56,512]{2,1,0:T(8,128)S(1)}, f32[4,56,512]{2,1,0:T(8,128)S(1)}, u32[]{:S(2)}, u32[]{:S(2)}) %collective-permute-start.5) | collective-permute-done | bytes 458784 | tf_op jit(solution)/shard_map/ppermute | solution.py:23
  90.5 3.2 %collective-permute-start.9 = (f32[56,512]{1,0:T(8,128)S(1)}, f32[56,512]{1,0:T(8,128)S(1)}, u32[]{:S(2)}, u32[]{:S(2)}) collective-permute-start(f32[56,512]{1,0:T(8,128)S(1)} %get-tuple-element.51), channel_id=1, source_target_pairs={{0,24},{8,0},{16,8},{24,16},{1,25},{9,1},{17,9},{25,17},{2,26},{10... | collective-permute-start | bytes 344072 | tf_op jit(solution)/shard_map/ppermute | solution.py:23
  94.4 2.5 %collective-permute-done.8 = f32[56,512]{1,0:T(8,128)S(1)} collective-permute-done((f32[56,512]{1,0:T(8,128)S(1)}, f32[56,512]{1,0:T(8,128)S(1)}, u32[]{:S(2)}, u32[]{:S(2)}) %collective-permute-start.8) | collective-permute-done | bytes 114720 | tf_op jit(solution)/shard_map/ppermute | solution.py:23
  97.3 2.7 %collective-permute-done.7 = f32[56,512]{1,0:T(8,128)S(1)} collective-permute-done((f32[56,512]{1,0:T(8,128)S(1)}, f32[56,512]{1,0:T(8,128)S(1)}, u32[]{:S(2)}, u32[]{:S(2)}) %collective-permute-start.7) | collective-permute-done | bytes 114720 | tf_op jit(solution)/shard_map/ppermute | solution.py:23
  100.1 0.8 maximum_multiply_fusion
  (34 shorter events, 2.0 us)
Async XLA Ops:
  4.3 12.5 %collective-permute-start = (f32[4,56,512]{2,1,0:T(8,128)}, f32[4,56,512]{2,1,0:T(8,128)S(1)}, u32[]{:S(2)}, u32[]{:S(2)}) collective-permute-start(f32[4,56,512]{2,1,0:T(8,128)} %get-tuple-element.32), channel_id=1, source_target_pairs={{0,32},{1,225},{2,34},{3,227},{4,36},{5,229},{6,38},{7,231},{32,64... | collective-permute-start | bytes 1376264 | tf_op jit(solution)/shard_map/ppermute | solution.py:33
  19.1 42.0 %collective-permute-start.2 = (f32[4,56,512]{2,1,0:T(8,128)}, f32[4,56,512]{2,1,0:T(8,128)}, u32[]{:S(2)}, u32[]{:S(2)}) collective-permute-start(f32[4,56,512]{2,1,0:T(8,128)} %get-tuple-element.44), channel_id=1, source_target_pairs={{0,224},{32,0},{64,32},{96,64},{128,96},{160,128},{192,160},{224,1... | collective-permute-start | bytes 1376264 | tf_op jit(solution)/shard_map/ppermute | solution.py:23
  21.1 39.9 %collective-permute-start.1 = (f32[4,56,512]{2,1,0:T(8,128)}, f32[4,56,512]{2,1,0:T(8,128)}, u32[]{:S(2)}, u32[]{:S(2)}) collective-permute-start(f32[4,56,512]{2,1,0:T(8,128)} %get-tuple-element.45), channel_id=1, source_target_pairs={{0,32},{32,64},{64,96},{96,128},{128,160},{160,192},{192,224},{224... | collective-permute-start | bytes 1376264 | tf_op jit(solution)/shard_map/ppermute | solution.py:23
  21.1 19.2 %copy-start.2 = (f32[1,512]{1,0:T(1,128)S(1)}, f32[1,512]{1,0:T(1,128)}, u32[]{:S(2)}) copy-start(f32[1,512]{1,0:T(1,128)} %get-tuple-element.43.q_ref) | copy-start | bytes 6148
  21.1 39.9 %copy-start.3 = (f32[4,4,56,512]{3,2,1,0:T(8,128)S(1)}, f32[4,4,56,512]{3,2,1,0:T(8,128)}, u32[]{:S(2)}) copy-start(f32[4,4,56,512]{3,2,1,0:T(8,128)} %get-tuple-element.31) | copy-start | bytes 5505028
  28.9 11.4 %all-to-all-start = ((f32[8,4,2048]{2,1,0:T(4,128)}), f32[8,4,2048]{2,1,0:T(4,128)S(1)}, u32[]{:S(2)}, u32[]{:S(2)}) async-start(f32[8,4,2048]{2,1,0:T(4,128)} %get-tuple-element.41), calls=%async_computation | async-start | bytes 524288 | tf_op jit(solution)/shard_map/all_to_all | solution.py:37
  33.9 8.1 %collective-permute-start.10 = (f32[8,8,512]{2,1,0:T(8,128)}, f32[8,8,512]{2,1,0:T(8,128)S(1)}, u32[]{:S(2)}, u32[]{:S(2)}) collective-permute-start(f32[8,8,512]{2,1,0:T(8,128)} %get-tuple-element.38), channel_id=1, source_target_pairs={{0,16},{8,24},{16,0},{24,8},{1,17},{9,25},{17,1},{25,9},{2,18},{10... | collective-permute-start | bytes 393224 | tf_op jit(solution)/shard_map/ppermute | solution.py:23
  37.1 7.9 %collective-permute-start.11 = (f32[8,8,512]{2,1,0:T(8,128)}, f32[8,8,512]{2,1,0:T(8,128)S(1)}, u32[]{:S(2)}, u32[]{:S(2)}) collective-permute-start(f32[8,8,512]{2,1,0:T(8,128)} %get-tuple-element.39), channel_id=1, source_target_pairs={{0,8},{8,16},{16,24},{24,0},{1,9},{9,17},{17,25},{25,1},{2,10},{10... | collective-permute-start | bytes 393224 | tf_op jit(solution)/shard_map/ppermute | solution.py:23
  37.8 7.9 %collective-permute-start.12 = (f32[8,8,512]{2,1,0:T(8,128)}, f32[8,8,512]{2,1,0:T(8,128)S(1)}, u32[]{:S(2)}, u32[]{:S(2)}) collective-permute-start(f32[8,8,512]{2,1,0:T(8,128)} %get-tuple-element.40), channel_id=1, source_target_pairs={{0,24},{8,0},{16,8},{24,16},{1,25},{9,1},{17,9},{25,17},{2,26},{10... | collective-permute-start | bytes 393224 | tf_op jit(solution)/shard_map/ppermute | solution.py:23
  40.3 0.7 copy-start.1
  42.0 6.9 %collective-permute-start.15 = (f32[64,512]{1,0:T(8,128)S(1)}, f32[64,512]{1,0:T(8,128)S(1)}, u32[]{:S(2)}, u32[]{:S(2)}) collective-permute-start(f32[64,512]{1,0:T(8,128)S(1)} %small_sums.1.refs_4_), channel_id=1, source_target_pairs={{0,24},{8,0},{16,8},{24,16},{1,25},{9,1},{17,9},{25,17},{2,26},{10... | collective-permute-start | bytes 393224 | tf_op jit(solution)/shard_map/ppermute | solution.py:23
  45.0 8.5 %collective-permute-start.14 = (f32[64,512]{1,0:T(8,128)S(1)}, f32[64,512]{1,0:T(8,128)S(1)}, u32[]{:S(2)}, u32[]{:S(2)}) collective-permute-start(f32[64,512]{1,0:T(8,128)S(1)} %small_sums.1.refs_4_), channel_id=1, source_target_pairs={{0,8},{8,16},{16,24},{24,0},{1,9},{9,17},{17,25},{25,1},{2,10},{10... | collective-permute-start | bytes 393224 | tf_op jit(solution)/shard_map/ppermute | solution.py:23
  45.7 7.8 %collective-permute-start.13 = (f32[64,512]{1,0:T(8,128)S(1)}, f32[64,512]{1,0:T(8,128)S(1)}, u32[]{:S(2)}, u32[]{:S(2)}) collective-permute-start(f32[64,512]{1,0:T(8,128)S(1)} %small_sums.1.refs_4_), channel_id=1, source_target_pairs={{0,16},{8,24},{16,0},{24,8},{1,17},{9,25},{17,1},{25,9},{2,18},{10... | collective-permute-start | bytes 393224 | tf_op jit(solution)/shard_map/ppermute | solution.py:23
  53.5 0.9 copy-start
  55.1 23.9 %copy-start.4 = (f32[3,4,56,512]{3,2,1,0:T(8,128)S(1)}, f32[3,4,56,512]{3,2,1,0:T(8,128)}, u32[]{:S(2)}) copy-start(f32[3,4,56,512]{3,2,1,0:T(8,128)} %get-tuple-element.30) | copy-start | bytes 4128772
  55.1 17.6 %all-to-all-start.1 = ((f32[8,16,512]{2,1,0:T(8,128)}), f32[8,16,512]{2,1,0:T(8,128)S(1)}, u32[]{:S(2)}, u32[]{:S(2)}) async-start(f32[8,16,512]{2,1,0:T(8,128)} %joined.1), calls=%async_computation.1 | async-start | bytes 524288 | tf_op jit(solution)/shard_map/all_to_all | solution.py:37
  63.3 13.8 %collective-permute-start.4 = (f32[4,56,512]{2,1,0:T(8,128)}, f32[4,56,512]{2,1,0:T(8,128)S(1)}, u32[]{:S(2)}, u32[]{:S(2)}) collective-permute-start(f32[4,56,512]{2,1,0:T(8,128)} %get-tuple-element.46), channel_id=1, source_target_pairs={{0,224},{32,0},{64,32},{96,64},{128,96},{160,128},{192,160},{224,1... | collective-permute-start | bytes 1376264 | tf_op jit(solution)/shard_map/ppermute | solution.py:23
  66.6 12.4 %collective-permute-start.3 = (f32[4,56,512]{2,1,0:T(8,128)}, f32[4,56,512]{2,1,0:T(8,128)S(1)}, u32[]{:S(2)}, u32[]{:S(2)}) collective-permute-start(f32[4,56,512]{2,1,0:T(8,128)} %get-tuple-element.47), channel_id=1, source_target_pairs={{0,32},{32,64},{64,96},{96,128},{128,160},{160,192},{192,224},{224... | collective-permute-start | bytes 1376264 | tf_op jit(solution)/shard_map/ppermute | solution.py:23
  79.2 11.1 %collective-permute-start.5 = (f32[4,56,512]{2,1,0:T(8,128)S(1)}, f32[4,56,512]{2,1,0:T(8,128)S(1)}, u32[]{:S(2)}, u32[]{:S(2)}) collective-permute-start(f32[4,56,512]{2,1,0:T(8,128)S(1)} %get-tuple-element.48), channel_id=1, source_target_pairs={{0,32},{32,64},{64,96},{96,128},{128,160},{160,192},{192,224},{224... | collective-permute-start | bytes 1376264 | tf_op jit(solution)/shard_map/ppermute | solution.py:23
  79.3 11.0 %collective-permute-start.6 = (f32[4,56,512]{2,1,0:T(8,128)S(1)}, f32[4,56,512]{2,1,0:T(8,128)S(1)}, u32[]{:S(2)}, u32[]{:S(2)}) collective-permute-start(f32[4,56,512]{2,1,0:T(8,128)S(1)} %get-tuple-element.49), channel_id=1, source_target_pairs={{0,224},{32,0},{64,32},{96,64},{128,96},{160,128},{192,160},{224,1... | collective-permute-start | bytes 1376264 | tf_op jit(solution)/shard_map/ppermute | solution.py:23
  90.5 6.5 %collective-permute-start.8 = (f32[56,512]{1,0:T(8,128)S(1)}, f32[56,512]{1,0:T(8,128)S(1)}, u32[]{:S(2)}, u32[]{:S(2)}) collective-permute-start(f32[56,512]{1,0:T(8,128)S(1)} %get-tuple-element.50), channel_id=1, source_target_pairs={{0,8},{8,16},{16,24},{24,0},{1,9},{9,17},{17,25},{25,1},{2,10},{10... | collective-permute-start | bytes 344072 | tf_op jit(solution)/shard_map/ppermute | solution.py:23
  90.5 6.8 %collective-permute-start.9 = (f32[56,512]{1,0:T(8,128)S(1)}, f32[56,512]{1,0:T(8,128)S(1)}, u32[]{:S(2)}, u32[]{:S(2)}) collective-permute-start(f32[56,512]{1,0:T(8,128)S(1)} %get-tuple-element.51), channel_id=1, source_target_pairs={{0,24},{8,0},{16,8},{24,16},{1,25},{9,1},{17,9},{25,17},{2,26},{10... | collective-permute-start | bytes 344072 | tf_op jit(solution)/shard_map/ppermute | solution.py:23
  93.8 6.3 %collective-permute-start.7 = (f32[56,512]{1,0:T(8,128)S(1)}, f32[56,512]{1,0:T(8,128)S(1)}, u32[]{:S(2)}, u32[]{:S(2)}) collective-permute-start(f32[56,512]{1,0:T(8,128)S(1)} %get-tuple-element.52), channel_id=1, source_target_pairs={{0,16},{8,24},{16,0},{24,8},{1,17},{9,25},{17,1},{25,9},{2,18},{10... | collective-permute-start | bytes 344072 | tf_op jit(solution)/shard_map/ppermute | solution.py:23
